TPU v7x, 128 devices: a whole 4x4x4 slice. The times are simulated.
128 devices in a mesh: batch: 8 (over z, y_hi), seq: 16 (over x, y_lo, core).
Axes of the slice: x: 4, y: 4 (y_hi: 2, y_lo: 2; y = y_hi * 2 + y_lo), z: 4, core: 2. Of those that a mesh axis runs over, the one named last changes fastest.
Arguments:
- tokens: bfloat16 [40960, 8192], P(('batch', 'seq')), may hold values from -24 to 24
- out_grad: bfloat16 [40960, 8192], P(('batch', 'seq')), may hold values from -0.109375 to 0.109375
- gate_pre: bfloat16 [40960, 768], P(('batch', 'seq')), may hold values from -8 to 8
- up_pre: bfloat16 [40960, 768], P(('batch', 'seq')), may hold values from -6 to 6
- hidden_grad: bfloat16 [40960, 768], P(('batch', 'seq')), may hold values from -0.03125 to 0.03125
Outputs:
- gate_weight_grad: float32 [8192, 768], P(('seq', 'batch'))
- up_weight_grad: float32 [8192, 768], P(('seq', 'batch'))
- down_weight_grad: float32 [8192, 768], P(('seq', 'batch'))
All inputs are finite; a program needn't handle non-finite values.
Results may differ from a plain program's by a relative error of at most 0.019.
Values may be sent and summed in bfloat16 or wider, within the bound.
A program may use at most 192 MiB of HBM per device.

v0:
```python
import jax
import jax.numpy as jnp
from jax import lax
from jax.sharding import Mesh
from jax.sharding import PartitionSpec as P

BATCH = ("batch_0", "batch_1")
BATCH_SEQ = ("batch_0", "batch_1", "seq")
SEQ_BATCH = ("seq", "batch_0", "batch_1")


def in_one_piece(arrays, axis, dim, along):
    ends, at = ([], 0)
    for a in arrays[:-1]:
        at += a.shape[along]
        ends.append(at)
    both = jnp.concatenate(arrays, axis=along)
    return tuple(jnp.split(lax.all_gather(both, axis, axis=dim, tiled=True), ends, axis=along))


def scatter_axes(x, axes, dim):
    for axis in axes:
        x = lax.psum_scatter(x, axis, scatter_dimension=dim, tiled=True)
    return x


def hidden_parts(gate_pre, up_pre, hidden_grad):
    gate_val = gate_pre.astype(jnp.float32)
    up_val = up_pre.astype(jnp.float32)
    grad_val = hidden_grad.astype(jnp.float32)
    sigmoid_val = jax.nn.sigmoid(gate_val)
    activated = gate_val * sigmoid_val
    hidden = (activated * up_val).astype(jnp.bfloat16)
    up_cotangent = (grad_val * activated).astype(jnp.bfloat16)
    gate_cotangent = (
        grad_val * up_val * sigmoid_val * (1.0 + gate_val * (1.0 - sigmoid_val))
    ).astype(jnp.bfloat16)
    return (hidden, gate_cotangent, up_cotangent)


def contract_rows(left, right):
    return lax.dot_general(
        left, right, (((0,), (0,)), ((), ())), preferred_element_type=jnp.float32
    )


def on_device(tokens, out_grad, gate_pre, up_pre, hidden_grad):
    hidden, gate_cotangent, up_cotangent = hidden_parts(gate_pre, up_pre, hidden_grad)
    cotangents = jnp.concatenate([gate_cotangent, up_cotangent], axis=1)
    model_width = tokens.shape[1]
    hidden_width = hidden.shape[1]
    seq_count = lax.axis_size("seq")
    own_rows = model_width // seq_count
    feature_block, grad_block = (
        lax.all_to_all(tokens, "seq", split_axis=1, concat_axis=0, tiled=True),
        lax.all_to_all(out_grad, "seq", split_axis=1, concat_axis=0, tiled=True),
    )
    cotangent_all, hidden_all = in_one_piece((cotangents, hidden), "seq", 0, 1)
    tok_rows = tokens.shape[0]

    def add_shard(shard_index, total):
        offset = shard_index * tok_rows
        features = lax.dynamic_slice_in_dim(feature_block, offset, tok_rows, 0)
        grads = lax.dynamic_slice_in_dim(grad_block, offset, tok_rows, 0)
        cotangent_rows = lax.dynamic_slice_in_dim(cotangent_all, offset, tok_rows, 0)
        hidden_slice = lax.dynamic_slice_in_dim(hidden_all, offset, tok_rows, 0)
        term = jnp.concatenate(
            [contract_rows(features, cotangent_rows), contract_rows(grads, hidden_slice)], axis=1
        )
        return total + lax.optimization_barrier(term.astype(jnp.bfloat16)).astype(jnp.float32)

    seq_total = lax.fori_loop(
        0, seq_count, add_shard, jnp.zeros((own_rows, 3 * hidden_width), jnp.float32)
    )
    group_total = scatter_axes(seq_total.astype(jnp.bfloat16), BATCH, 0).astype(jnp.float32)
    return (
        group_total[:, :hidden_width],
        group_total[:, hidden_width : 2 * hidden_width],
        group_total[:, 2 * hidden_width :],
    )


def solution(mesh):
    split = Mesh(mesh.devices.reshape(4, 2, mesh.shape["seq"]), ("batch_0", "batch_1", "seq"))
    in_specs = (
        P(BATCH_SEQ, None),
        P(BATCH_SEQ, None),
        P(BATCH_SEQ, None),
        P(BATCH_SEQ, None),
        P(BATCH_SEQ, None),
    )
    out_specs = (P(SEQ_BATCH, None), P(SEQ_BATCH, None), P(SEQ_BATCH, None))
    return jax.shard_map(
        on_device, mesh=split, in_specs=in_specs, out_specs=out_specs, check_vma=False
    )
```

profile of v0, /device:TPU:0, one launch (start us, length us, event | category | flops | bytes accessed | tf_op | source)
XLA Modules:
  0.0 479.7 jit_solution(2862090613700210809)
XLA Ops:
  10.4 5.3 %copy.15 = bf16[40,16,8,512]{3,2,0,1:T(8,128)(2,1)} copy(bf16[40,16,8,512]{3,2,1,0:T(8,128)(2,1)} %bitcast.16) | data formatting | bytes 10485760 | tf_op jit(solution)/shard_map/all_to_all | solution.py:55
  15.7 5.6 %all-to-all-start = ((bf16[320,16,512]{2,0,1:T(8,128)(2,1)}), bf16[320,16,512]{2,0,1:T(8,128)(2,1)}, u32[]{:S(2)}, u32[]{:S(2)}) async-start(bf16[320,16,512]{2,0,1:T(8,128)(2,1)} %bitcast.15), calls=%async_computation | async-start | bytes 10485760 | tf_op jit(solution)/shard_map/all_to_all | solution.py:55
  21.3 6.3 %copy.14 = bf16[40,16,8,512]{3,2,0,1:T(8,128)(2,1)} copy(bf16[40,16,8,512]{3,2,1,0:T(8,128)(2,1)} %bitcast.17) | data formatting | bytes 10485760 | tf_op jit(solution)/shard_map/all_to_all | solution.py:56
  27.6 102.8 %all-to-all-done = bf16[320,16,512]{2,0,1:T(8,128)(2,1)} async-done(((bf16[320,16,512]{2,0,1:T(8,128)(2,1)}), bf16[320,16,512]{2,0,1:T(8,128)(2,1)}, u32[]{:S(2)}, u32[]{:S(2)}) %all-to-all-start) | async-done | bytes 5242912 | tf_op jit(solution)/shard_map/all_to_all | solution.py:55
  130.4 13.1 %all-to-all-start.1 = ((bf16[320,16,512]{2,0,1:T(8,128)(2,1)}), bf16[320,16,512]{2,0,1:T(8,128)(2,1)}, u32[]{:S(2)}, u32[]{:S(2)}) async-start(bf16[320,16,512]{2,0,1:T(8,128)(2,1)} %bitcast.14), calls=%async_computation.1 | async-start | bytes 10485760 | tf_op jit(solution)/shard_map/all_to_all | solution.py:56
  143.5 105.5 %all-gather.2.cloned.1.call-done = bf16[5120,2304]{1,0:T(8,128)(2,1)} async-done(((bf16[320,2304]{1,0:T(8,128)(2,1)}), bf16[5120,2304]{1,0:T(8,128)(2,1)}) %all-gather.2.cloned.1.call-update) | async-done | bytes 23592976 | tf_op jit(solution)/shard_map/all_gather | solution.py:18
  249.0 13.1 %split.8 = bf16[5120,1536]{1,0:T(8,128)(2,1)} slice(bf16[5120,2304]{1,0:T(8,128)(2,1)} %all-gather.2.cloned.1.call-done), slice={[0:5120], [0:1536]} | slice | bytes 31457280 | tf_op jit(solution)/shard_map/split | solution.py:18
  262.1 6.9 %split.9 = bf16[5120,768]{1,0:T(8,128)(2,1)} slice(bf16[5120,2304]{1,0:T(8,128)(2,1)} %all-gather.2.cloned.1.call-done), slice={[0:5120], [1536:2304]} | slice | bytes 15728640 | tf_op jit(solution)/shard_map/split | solution.py:18
  269.1 144.5 %while.14 = (s32[]{:T(128)}, f32[512,2304]{1,0:T(8,128)}, bf16[5120,512]{1,0:T(8,128)(2,1)}, bf16[5120,1536]{1,0:T(8,128)(2,1)}, bf16[5120,512]{1,0:T(8,128)(2,1...) while((s32[]{:T(128)}, f32[512,2304]{1,0:T(8,128)}, ...), condition=%wide.region_1.0_spmd.clone, body=%wide.region_0.0_spmd.clone.sunk | while | flops 764411904 | bytes 21006492 | solution.py:72
  269.1 2.3 convolution_convert_fusion.5
  273.3 2.6 select_add_fusion.2
  280.1 5.0 %select_add_fusion.2 = f32[512,2304]{1,0:T(8,128)} fusion(f32[512,2304]{1,0:T(8,128)} %get-tuple-element.200, bf16[512,2304]{1,0:T(8,128)(2,1)S(1)} %pad_maximum_fusion.3, pred[]{:T(512)S(6)} %compare.3), kind=kLoop, calls=%fused_computation.clone.1 | loop fusion | flops 3538944 | bytes 11796481 | tf_op jit(solution)/shard_map/while/body/eval_jaxpr/add | solution.py:70
  285.1 2.3 convolution_convert_fusion.5
  289.3 5.0 %select_add_fusion.2 = f32[512,2304]{1,0:T(8,128)} fusion(f32[512,2304]{1,0:T(8,128)} %get-tuple-element.200, bf16[512,2304]{1,0:T(8,128)(2,1)S(1)} %pad_maximum_fusion.3, pred[]{:T(512)S(6)} %compare.3), kind=kLoop, calls=%fused_computation.clone.1 | loop fusion | flops 3538944 | bytes 11796481 | tf_op jit(solution)/shard_map/while/body/eval_jaxpr/add | solution.py:70
  298.5 5.0 %select_add_fusion.2 = f32[512,2304]{1,0:T(8,128)} fusion(f32[512,2304]{1,0:T(8,128)} %get-tuple-element.200, bf16[512,2304]{1,0:T(8,128)(2,1)S(1)} %pad_maximum_fusion.3, pred[]{:T(512)S(6)} %compare.3), kind=kLoop, calls=%fused_computation.clone.1 | loop fusion | flops 3538944 | bytes 11796481 | tf_op jit(solution)/shard_map/while/body/eval_jaxpr/add | solution.py:70
  303.4 2.3 convolution_convert_fusion.5
  307.7 5.0 %select_add_fusion.2 = f32[512,2304]{1,0:T(8,128)} fusion(f32[512,2304]{1,0:T(8,128)} %get-tuple-element.200, bf16[512,2304]{1,0:T(8,128)(2,1)S(1)} %pad_maximum_fusion.3, pred[]{:T(512)S(6)} %compare.3), kind=kLoop, calls=%fused_computation.clone.1 | loop fusion | flops 3538944 | bytes 11796481 | tf_op jit(solution)/shard_map/while/body/eval_jaxpr/add | solution.py:70
  316.8 5.0 %select_add_fusion.2 = f32[512,2304]{1,0:T(8,128)} fusion(f32[512,2304]{1,0:T(8,128)} %get-tuple-element.200, bf16[512,2304]{1,0:T(8,128)(2,1)S(1)} %pad_maximum_fusion.3, pred[]{:T(512)S(6)} %compare.3), kind=kLoop, calls=%fused_computation.clone.1 | loop fusion | flops 3538944 | bytes 11796481 | tf_op jit(solution)/shard_map/while/body/eval_jaxpr/add | solution.py:70
  326.0 5.0 %select_add_fusion.2 = f32[512,2304]{1,0:T(8,128)} fusion(f32[512,2304]{1,0:T(8,128)} %get-tuple-element.200, bf16[512,2304]{1,0:T(8,128)(2,1)S(1)} %pad_maximum_fusion.3, pred[]{:T(512)S(6)} %compare.3), kind=kLoop, calls=%fused_computation.clone.1 | loop fusion | flops 3538944 | bytes 11796481 | tf_op jit(solution)/shard_map/while/body/eval_jaxpr/add | solution.py:70
  335.2 5.0 %select_add_fusion.2 = f32[512,2304]{1,0:T(8,128)} fusion(f32[512,2304]{1,0:T(8,128)} %get-tuple-element.200, bf16[512,2304]{1,0:T(8,128)(2,1)S(1)} %pad_maximum_fusion.3, pred[]{:T(512)S(6)} %compare.3), kind=kLoop, calls=%fused_computation.clone.1 | loop fusion | flops 3538944 | bytes 11796481 | tf_op jit(solution)/shard_map/while/body/eval_jaxpr/add | solution.py:70
  344.4 5.0 %select_add_fusion.2 = f32[512,2304]{1,0:T(8,128)} fusion(f32[512,2304]{1,0:T(8,128)} %get-tuple-element.200, bf16[512,2304]{1,0:T(8,128)(2,1)S(1)} %pad_maximum_fusion.3, pred[]{:T(512)S(6)} %compare.3), kind=kLoop, calls=%fused_computation.clone.1 | loop fusion | flops 3538944 | bytes 11796481 | tf_op jit(solution)/shard_map/while/body/eval_jaxpr/add | solution.py:70
  353.6 5.0 %select_add_fusion.2 = f32[512,2304]{1,0:T(8,128)} fusion(f32[512,2304]{1,0:T(8,128)} %get-tuple-element.200, bf16[512,2304]{1,0:T(8,128)(2,1)S(1)} %pad_maximum_fusion.3, pred[]{:T(512)S(6)} %compare.3), kind=kLoop, calls=%fused_computation.clone.1 | loop fusion | flops 3538944 | bytes 11796481 | tf_op jit(solution)/shard_map/while/body/eval_jaxpr/add | solution.py:70
  358.5 2.3 convolution_convert_fusion.5
  362.7 5.0 %select_add_fusion.2 = f32[512,2304]{1,0:T(8,128)} fusion(f32[512,2304]{1,0:T(8,128)} %get-tuple-element.200, bf16[512,2304]{1,0:T(8,128)(2,1)S(1)} %pad_maximum_fusion.3, pred[]{:T(512)S(6)} %compare.3), kind=kLoop, calls=%fused_computation.clone.1 | loop fusion | flops 3538944 | bytes 11796481 | tf_op jit(solution)/shard_map/while/body/eval_jaxpr/add | solution.py:70
  371.9 5.0 %select_add_fusion.2 = f32[512,2304]{1,0:T(8,128)} fusion(f32[512,2304]{1,0:T(8,128)} %get-tuple-element.200, bf16[512,2304]{1,0:T(8,128)(2,1)S(1)} %pad_maximum_fusion.3, pred[]{:T(512)S(6)} %compare.3), kind=kLoop, calls=%fused_computation.clone.1 | loop fusion | flops 3538944 | bytes 11796481 | tf_op jit(solution)/shard_map/while/body/eval_jaxpr/add | solution.py:70
  381.1 5.0 %select_add_fusion.2 = f32[512,2304]{1,0:T(8,128)} fusion(f32[512,2304]{1,0:T(8,128)} %get-tuple-element.200, bf16[512,2304]{1,0:T(8,128)(2,1)S(1)} %pad_maximum_fusion.3, pred[]{:T(512)S(6)} %compare.3), kind=kLoop, calls=%fused_computation.clone.1 | loop fusion | flops 3538944 | bytes 11796481 | tf_op jit(solution)/shard_map/while/body/eval_jaxpr/add | solution.py:70
  390.3 5.0 %select_add_fusion.2 = f32[512,2304]{1,0:T(8,128)} fusion(f32[512,2304]{1,0:T(8,128)} %get-tuple-element.200, bf16[512,2304]{1,0:T(8,128)(2,1)S(1)} %pad_maximum_fusion.3, pred[]{:T(512)S(6)} %compare.3), kind=kLoop, calls=%fused_computation.clone.1 | loop fusion | flops 3538944 | bytes 11796481 | tf_op jit(solution)/shard_map/while/body/eval_jaxpr/add | solution.py:70
  399.5 5.0 %select_add_fusion.2 = f32[512,2304]{1,0:T(8,128)} fusion(f32[512,2304]{1,0:T(8,128)} %get-tuple-element.200, bf16[512,2304]{1,0:T(8,128)(2,1)S(1)} %pad_maximum_fusion.3, pred[]{:T(512)S(6)} %compare.3), kind=kLoop, calls=%fused_computation.clone.1 | loop fusion | flops 3538944 | bytes 11796481 | tf_op jit(solution)/shard_map/while/body/eval_jaxpr/add | solution.py:70
  408.6 5.0 %select_add_fusion.2 = f32[512,2304]{1,0:T(8,128)} fusion(f32[512,2304]{1,0:T(8,128)} %get-tuple-element.200, bf16[512,2304]{1,0:T(8,128)(2,1)S(1)} %pad_maximum_fusion.3, pred[]{:T(512)S(6)} %compare.3), kind=kLoop, calls=%fused_computation.clone.1 | loop fusion | flops 3538944 | bytes 11796481 | tf_op jit(solution)/shard_map/while/body/eval_jaxpr/add | solution.py:70
  413.6 4.0 convert_element_type.42
  417.6 32.4 %reduce-scatter.3.cloned.1.call-done = bf16[128,2304]{1,0:T(8,128)(2,1)} async-done(((bf16[512,2304]{1,0:T(8,128)(2,1)}), bf16[128,2304]{1,0:T(8,128)(2,1)}) %reduce-scatter.3.cloned.1.call-update) | async-done | bytes 589840 | tf_op jit(solution)/shard_map/reduce_scatter | solution.py:23
  450.0 21.4 %reduce-scatter.5.cloned.1.call-done = bf16[64,2304]{1,0:T(8,128)(2,1)} async-done(((bf16[128,2304]{1,0:T(8,128)(2,1)}), bf16[64,2304]{1,0:T(8,128)(2,1)}) %reduce-scatter.5.cloned.1.call-update) | async-done | bytes 294928 | tf_op jit(solution)/shard_map/reduce_scatter | solution.py:23
  (55 shorter events, 63.1 us)
Async XLA Ops:
  7.2 241.8 %all-gather.2.cloned.1.call-start = ((), (), s32[]{:S(2)}) async-start(), calls=%async_computation.4 | async-start | bytes 25067520 | tf_op jit(solution)/shard_map/all_gather | solution.py:18
  15.7 114.6 %all-to-all-start = ((bf16[320,16,512]{2,0,1:T(8,128)(2,1)}), bf16[320,16,512]{2,0,1:T(8,128)(2,1)}, u32[]{:S(2)}, u32[]{:S(2)}) async-start(bf16[320,16,512]{2,0,1:T(8,128)(2,1)} %bitcast.15), calls=%async_computation | async-start | bytes 10485760 | tf_op jit(solution)/shard_map/all_to_all | solution.py:55
  130.4 138.7 %all-to-all-start.1 = ((bf16[320,16,512]{2,0,1:T(8,128)(2,1)}), bf16[320,16,512]{2,0,1:T(8,128)(2,1)}, u32[]{:S(2)}, u32[]{:S(2)}) async-start(bf16[320,16,512]{2,0,1:T(8,128)(2,1)} %bitcast.14), calls=%async_computation.1 | async-start | bytes 10485760 | tf_op jit(solution)/shard_map/all_to_all | solution.py:56
  143.4 306.5 %reduce-scatter.3.cloned.1.call-start = ((), (), s32[]{:S(2)}) async-start(), calls=%async_computation.5 | async-start | bytes 2949120 | tf_op jit(solution)/shard_map/reduce_scatter | solution.py:23
  417.6 53.8 %reduce-scatter.5.cloned.1.call-start = ((), (), s32[]{:S(2)}) async-start(), calls=%async_computation.6 | async-start | bytes 884736 | tf_op jit(solution)/shard_map/reduce_scatter | solution.py:23
Sparse Core Ops, SparseCore 0:
  10.5 238.4 all-gather.1
  417.7 32.2 reduce-scatter.2
  452.4 18.9 reduce-scatter.4
where the time goes:
time: 482 us; the launch traced here: 480 us
  waiting for transfers between devices  262 us (54%)
  other arithmetic  86.5 us (18%)
  matrix products  64.7 us (13%)
  local copies, waits for them, and re-layouts  33.5 us (7%)
  starting transfers between devices  18.8 us (4%)
  between operations  13.8 us (3%)
    all_gather x1, waiting for transfers between devices, in_one_piece(): lax.all_gather(both, axis, axis=dim, tiled=True)  106 us
    all_to_all x1, waiting for transfers between devices, on_device(): lax.all_to_all(tokens, 'seq', split_axis=1, concat_axis=0, tiled=True)  103 us
    add x16, other arithmetic, add_shard(): total + lax.optimization_barrier(term.astype(jnp.bfloat16)).astype(jnp.fl...  76.9 us
    dot_general x32, matrix products, contract_rows(): lax.dot_general(left, right, (((0,), (0,)), ((), ())), preferred_element_...  64.7 us
    reduce_scatter x2, waiting for transfers between devices, scatter_axes(): x = lax.psum_scatter(x, axis, scatter_dimension=dim, tiled=True)  53.7 us
    split x2, local copies, waits for them, and re-layouts, in_one_piece(): jnp.split(lax.all_gather(both, axis, axis=dim, tiled=True), ends, axis=al...  20.1 us
    all_to_all x1, starting transfers between devices, on_device(): lax.all_to_all(out_grad, 'seq', split_axis=1, concat_axis=0, tiled=True)  13.1 us
  transfers between devices with their start and end apart: 5, of which 4 were waited for; matrix products, arithmetic and copies ran while one was open for 7% of the time, Pallas kernels for 0%

commit v1 on v0

v1 whole, which is shorter than its diff:
```python
import functools

import jax
import jax.numpy as jnp
from jax import lax
from jax.experimental import pallas as pl
from jax.experimental.pallas import tpu as pltpu
from jax.sharding import Mesh
from jax.sharding import PartitionSpec as P

AXES = ("z", "yh", "x", "yl", "c")
ORDERS = ("xyz", "yzx", "zxy")
MESH = pl.DeviceIdType.MESH
F32, BF16 = jnp.float32, jnp.bfloat16

SUBS = 3
def schedule():
    s = []
    for p in range(3):
        s.append(("C", p, 0, 0))
    for p in range(3):
        s.append(("C", p, 1, 0))
    for p in range(3):
        s += [("E1", p, 0, 0), ("M", p, 1, 0)]
    for p in range(3):
        s.append(("C", p, 2, 0))
    for p in range(3):
        s += [("E2", p, 0, 0), ("M", p, 0, 1)]
    for p in range(3):
        s += [("E1", p, 1, 0), ("M", p, 2, 0)]
    for p in range(3):
        s += [("E1", p, 0, 1)]
    for p in range(3):
        s += [("E2", p, 0, 1), ("M", p, 0, 2)]
    for p in range(3):
        s += [("E2", p, 1, 0), ("M", p, 1, 1)]
    for p in range(3):
        s += [("E1", p, 0, 2)]
    for p in range(3):
        s += [("E2", p, 0, 2)]
    for p in range(3):
        s += [("E1", p, 2, 0)]
    for p in range(3):
        s += [("E1", p, 1, 1)]
    for p in range(3):
        s += [("E2", p, 1, 1), ("M", p, 1, 2)]
    for p in range(3):
        s += [("E1", p, 1, 2)]
    for p in range(3):
        s += [("E2", p, 1, 2)]
    for ph in range(3):
        if ph:
            for p in range(3):
                s += [("E1", p, 2, ph)]
        for p in range(3):
            s += [("E2", p, 2, ph)]
            if ph < 2:
                s += [("M", p, 2, ph + 1)]
    return s


def kernel(tokens, out_grad, gate_pre, up_pre, hidden_grad, out0, out1, out2,
           tok, raw, hb, part, r0, r1, r2, send_sem, recv_sem, in_sem, xs_sem, xr_sem):
    outs = (out0, out1, out2)
    recv = (r0, r1, r2)
    z, yh, x, yl, c = (lax.axis_index(a) for a in AXES)
    y = yh * 2 + yl
    me = {"x": x, "y": y, "z": z}
    n_tok = tokens.shape[0]
    cols = hb.shape[3]
    tile = tok.shape[3]
    n_tile = tok.shape[1]
    rows = part.shape[5]
    step = {}
    for d in "xyz":
        step[d] = tuple(lax.rem(me[d] + k, 4) for k in range(4))

    def device(d, k):
        at = dict(me)
        at[d] = step[d][k]
        return (at["z"], lax.div(at["y"], 2), at["x"], lax.rem(at["y"], 2), c)

    partner = (z, yh, x, yl, 1 - c)

    own = []
    raws = (gate_pre, up_pre, hidden_grad)
    for i, ref in enumerate(raws):
        own.append(pltpu.make_async_copy(ref, raw.at[i, pl.ds(0, n_tok)], in_sem.at[i]))
    bigs = (tokens, out_grad)
    for w, ref in enumerate(bigs):
        for m in range(n_tile):
            at = pl.multiple_of((m * 2 + c) * tile, tile)
            own.append(pltpu.make_async_copy(
                ref.at[:, pl.ds(at, tile)], tok.at[w, m, pl.ds(0, n_tok)], in_sem.at[3 + w * n_tile + m]))
    for cp in own:
        cp.start()

    barrier = pltpu.get_barrier_semaphore()
    pl.semaphore_signal(barrier, inc=1, device_id=partner, device_id_type=MESH)
    for d in "xyz":
        for k in (1, 3):
            pl.semaphore_signal(barrier, inc=1, device_id=device(d, k), device_id_type=MESH)
    pl.semaphore_wait(barrier, 7)

    swap = []
    for i, ref in enumerate(raws):
        swap.append(pltpu.make_async_remote_copy(
            ref, raw.at[i, pl.ds(n_tok, n_tok)], xs_sem.at[i], xr_sem.at[i],
            device_id=partner, device_id_type=MESH))
    for w, ref in enumerate(bigs):
        for m in range(n_tile):
            at = pl.multiple_of((m * 2 + 1 - c) * tile, tile)
            swap.append(pltpu.make_async_remote_copy(
                ref.at[:, pl.ds(at, tile)], tok.at[w, m, pl.ds(n_tok, n_tok)],
                xs_sem.at[3 + w * n_tile + m], xr_sem.at[3 + w * n_tile + m],
                device_id=partner, device_id_type=MESH))
    for cp in swap:
        cp.start()

    piece = 32

    def hidden(j):
        def body(i, carry):
            at = pl.ds(pl.multiple_of(i * piece, piece), piece)
            cs = pl.ds(j * cols, cols)
            gate_val = raw[0, at, cs].astype(F32)
            up_val = raw[1, at, cs].astype(F32)
            grad_val = raw[2, at, cs].astype(F32)
            sig = jax.nn.sigmoid(gate_val)
            activated = gate_val * sig
            hb[2, j, at] = (activated * up_val).astype(BF16)
            hb[1, j, at] = (grad_val * activated).astype(BF16)
            hb[0, j, at] = (grad_val * up_val * sig * (1.0 + gate_val * (1.0 - sig))).astype(BF16)
            return carry
        return body

    descs = {}

    def base(p, j, ph):
        o = ORDERS[p]
        ref = part.at[p, j]
        if ph >= 1:
            ref = ref.at[me[o[0]]]
        if ph >= 2:
            ref = ref.at[me[o[1]]]
        return ref

    def half_of(ref, k, h):
        n = ref.shape[1] // 2
        return ref.at[k, pl.ds(h * n, n)]

    def message(p, j, ph, i, src, direction):
        d = ORDERS[p][ph]
        cp = pltpu.make_async_remote_copy(
            src, recv[ph].at[p, j, i], send_sem.at[p, j, ph, i], recv_sem.at[p, j, ph, i],
            device_id=device(d, direction), device_id_type=MESH)
        cp.start()
        descs[(p, j, ph, i)] = cp

    def send_far(p, j, ph):
        b = base(p, j, ph)
        s = step[ORDERS[p][ph]]
        message(p, j, ph, 0, half_of(b, s[2], 0), 1)
        message(p, j, ph, 1, half_of(b, s[2], 1), 3)

    def send_near(p, j, ph):
        b = base(p, j, ph)
        s = step[ORDERS[p][ph]]
        message(p, j, ph, 2, half_of(b, s[1], 1), 1)
        message(p, j, ph, 3, half_of(b, s[3], 0), 3)

    arrived = set()

    def need(key, copies):
        if key not in arrived:
            arrived.add(key)
            for cp in copies:
                cp()

    def matmul(p, j, ms):
        w = 1 if p == 2 else 0
        o = ORDERS[p]

        def one(m):
            res = lax.dot_general(tok[w, m], hb[p, j], (((0,), (0,)), ((), ())),
                                  preferred_element_type=F32).astype(BF16)
            mx = lax.div(m, 2)
            ml = lax.rem(m, 2)
            for zz in range(4):
                for hh in range(2):
                    at = {"x": mx, "y": hh * 2 + ml, "z": zz}
                    lo = (zz * 2 + hh) * rows
                    part[p, j, at[o[0]], at[o[1]], at[o[2]]] = res[lo:lo + rows]

        n, f = ms

        def body(i, carry):
            one(f(i))
            return carry
        lax.fori_loop(0, n, body, 0)

    def compute(p, j, send):
        if p == 0:
            if j == 0:
                for i in range(3):
                    own[i].wait()
                    swap[i].wait_recv()
            lax.fori_loop(0, 2 * n_tok // piece, hidden(j), 0)
        if j == 0 and p in (0, 2):
            w = p // 2
            for m in range(n_tile):
                own[3 + w * n_tile + m].wait()
                swap[3 + w * n_tile + m].wait_recv()
        if p == 0 and send:
            s = step["x"]
            matmul(p, j, (2, lambda i: s[2] * 2 + i))
            send_far(p, j, 0)
            matmul(p, j, (4, lambda i: lax.rem(s[1] + 2 * lax.div(i, 2), 4) * 2 + lax.rem(i, 2)))
            send_near(p, j, 0)
            matmul(p, j, (2, lambda i: s[0] * 2 + i))
        elif p == 1 and send:
            matmul(p, j, (4, lambda i: i * 2 + yl))
            send_far(p, j, 0)
            matmul(p, j, (4, lambda i: i * 2 + 1 - yl))
            send_near(p, j, 0)
        else:
            matmul(p, j, (n_tile, lambda i: i))
            if send:
                send_far(p, j, 0)
                send_near(p, j, 0)

    def relay(p, j, ph):
        b = base(p, j, ph)
        s = step[ORDERS[p][ph]]
        for i, k in ((0, 1), (1, 3)):
            descs[(p, j, ph, i)].wait_recv()
            got = recv[ph].at[p, j, i]
            mine = half_of(b, s[k], i)
            add(got, (mine,), got)
            message(p, j, ph, 4 + i, got, k)

    def add(first, others, dst):
        shape = dst.shape
        lead = shape[:-2]
        count = 1
        for n in lead:
            count *= n

        def block(ix):
            v = first[ix].astype(F32)
            for o in others:
                v = v + o[ix].astype(F32)
            dst[ix] = v.astype(dst.dtype)

        if count == 1 and not lead:
            block((slice(None), slice(None)))
            return

        def body(i, carry):
            if len(lead) == 1:
                block((i,))
            else:
                block((lax.div(i, lead[1]), lax.rem(i, lead[1])))
            return carry
        lax.fori_loop(0, count, body, 0)

    def finish(p, j, ph):
        b = base(p, j, ph)
        s = step[ORDERS[p][ph]]
        for i in (2, 3, 4, 5):
            descs[(p, j, ph, i)].wait_recv()
        got = recv[ph]
        for h, (i, k) in enumerate(((3, 4), (2, 5))):
            mine = half_of(b, s[0], h)
            if ph < 2:
                dst = mine
            else:
                n = rows // 2
                dst = outs[p].at[pl.ds(h * n, n), pl.ds(j * cols, cols)]
            add(mine, (got.at[p, j, i], got.at[p, j, k]), dst)

    for op, p, j, ph in schedule():
        if op == "C":
            compute(p, j, j == 0)
        elif op == "M":
            send_far(p, j, ph)
            send_near(p, j, ph)
        elif op == "E1":
            relay(p, j, ph)
        else:
            finish(p, j, ph)

    for cp in swap:
        cp.wait_send()
    for cp in descs.values():
        cp.wait_send()


def on_device(tokens, out_grad, gate_pre, up_pre, hidden_grad):
    n_tok, width = tokens.shape
    hid = gate_pre.shape[1]
    rows = width // 128
    cols = hid // SUBS
    tile = width // 16
    dma = pltpu.SemaphoreType.DMA
    any_spec = pl.BlockSpec(memory_space=pl.ANY)
    vmem = pl.BlockSpec(memory_space=pltpu.VMEM)
    out = jax.ShapeDtypeStruct((rows, hid), F32)
    n_in = 3 + 16
    return pl.pallas_call(
        kernel,
        out_shape=(out,) * 3,
        in_specs=[any_spec] * 5,
        out_specs=(vmem,) * 3,
        scratch_shapes=[
            pltpu.VMEM((2, 8, 2 * n_tok, tile), BF16),
            pltpu.VMEM((3, 2 * n_tok, hid), BF16),
            pltpu.VMEM((3, SUBS, 2 * n_tok, cols), BF16),
            pltpu.VMEM((3, SUBS, 4, 4, 4, rows, cols), BF16),
            pltpu.VMEM((3, SUBS, 6, 2, 4, rows, cols), BF16),
            pltpu.VMEM((3, SUBS, 6, 2, rows, cols), BF16),
            pltpu.VMEM((3, SUBS, 6, rows // 2, cols), BF16),
            dma((3, SUBS, 3, 6)),
            dma((3, SUBS, 3, 6)),
            dma((n_in,)),
            dma((n_in,)),
            dma((n_in,)),
        ],
        compiler_params=pltpu.CompilerParams(
            collective_id=0, has_side_effects=True, vmem_limit_bytes=67043328),
        name="grad_sum",
    )(tokens, out_grad, gate_pre, up_pre, hidden_grad)


def solution(mesh):
    split = Mesh(mesh.devices.reshape(4, 2, 4, 2, 2), AXES)
    spec_in = P(AXES, None)
    spec_out = P(("x", "yl", "c", "z", "yh"), None)
    return jax.shard_map(
        on_device, mesh=split, in_specs=(spec_in,) * 5, out_specs=(spec_out,) * 3, check_vma=False
    )
```

time: 482 us -> 124 us (0.26)
  waiting for transfers between devices: 262 us -> 0 us
  Pallas kernels: 0 us -> 118 us
  other arithmetic: 86.5 us -> 0 us
  matrix products: 64.7 us -> 0 us
  local copies, waits for them, and re-layouts: 33.5 us -> 4.85 us
  starting transfers between devices: 18.8 us -> 0 us
  between operations: 13.8 us -> 0.64 us
    pallas_call x0 -> x1, Pallas kernels: none -> 118 us  [on_device(): pl.pallas_call(kernel, out_shape=(out,) * 3, in_specs=[any_spec] * 5, out...]
    all_gather x1 -> x0, waiting for transfers between devices: 106 us -> none  [in_one_piece(): lax.all_gather(both, axis, axis=dim, tiled=True)]
    all_to_all x2 -> x0, waiting for transfers between devices: 103 us -> none  [the longest x1 103 us: on_device(): lax.all_to_all(tokens, 'seq', split_axis=1, concat_axis=0, tiled=True)]
    add x16 -> x0, other arithmetic: 76.9 us -> none  [add_shard(): total + lax.optimization_barrier(term.astype(jnp.bfloat16)).astype(jnp.fl...]
    dot_general x32 -> x0, matrix products: 64.7 us -> none  [contract_rows(): lax.dot_general(left, right, (((0,), (0,)), ((), ())), preferred_element_...]
    reduce_scatter x2 -> x0, waiting for transfers between devices: 53.7 us -> none  [scatter_axes(): x = lax.psum_scatter(x, axis, scatter_dimension=dim, tiled=True)]
    split x2 -> x0, local copies, waits for them, and re-layouts: 20.1 us -> none  [in_one_piece(): jnp.split(lax.all_gather(both, axis, axis=dim, tiled=True), ends, axis=al...]
    all_to_all x2 -> x0, starting transfers between devices: 18.7 us -> none  [the longest x1 13.1 us: on_device(): lax.all_to_all(out_grad, 'seq', split_axis=1, concat_axis=0, tiled=True)]
  transfers between devices with their start and end apart: 5 -> 0, of which waited for: 4 -> 0; matrix products, arithmetic and copies ran while one was open for 7% -> 0% of each run, Pallas kernels for 0% -> 0%
where the time goes in v1:
time: 124 us
  Pallas kernels  118 us (95%)
  local copies, waits for them, and re-layouts  4.85 us (4%)
    pallas_call x1, Pallas kernels, on_device(): pl.pallas_call(kernel, out_shape=(out,) * 3, in_specs=[any_spec] * 5, out...  118 us
    unnamed x3, local copies, waits for them, and re-layouts  4.85 us

profile of v1, /device:TPU:0, one launch (start us, length us, event | category | flops | bytes accessed | tf_op | source)
XLA Modules:
  0.0 124.0 jit_solution(304762793432249322)
XLA Ops:
  0.6 118.5 %grad_sum.1 = (f32[64,768]{1,0:T(8,128)}, f32[64,768]{1,0:T(8,128)}, f32[64,768]{1,0:T(8,128)}) custom-call(bf16[320,8192]{1,0:T(8,128)(2,1)} %tokens.1, bf16[320,8192]{1,0:T(8,128)(2,1)} %out_grad.1, bf16[320,768]{1,0:T(8,128)(2,1)} %gate_pre.1, bf16[320,768]{1,0:T(8,128)(2,1)} %up_pre.1, bf16[320,768]{1,0:T(8,128)(2,1)} %hidden_grad.1), custom_call_target="tpu_custom_call" | custom-call | tf_op jit(solution)/shard_map/grad_sum/pallas_call | solution.py:310
  119.1 1.6 %copy.11 = f32[64,768]{1,0:T(8,128)} copy(f32[64,768]{1,0:T(8,128)} %get-tuple-element.6) | data formatting | bytes 393216
  120.7 1.6 %copy.12 = f32[64,768]{1,0:T(8,128)} copy(f32[64,768]{1,0:T(8,128)} %get-tuple-element.7) | data formatting | bytes 393216
  122.3 1.6 %copy.13 = f32[64,768]{1,0:T(8,128)} copy(f32[64,768]{1,0:T(8,128)} %get-tuple-element.8) | data formatting | bytes 393216

commit v2 on v0

v2 whole, which is shorter than its diff:
```python
import jax
import jax.numpy as jnp
from jax import lax
from jax.experimental import pallas as pl
from jax.experimental.pallas import tpu as pltpu
from jax.sharding import Mesh
from jax.sharding import PartitionSpec as P

AXES = ("z", "yh", "x", "yl", "c")
DIM_ORDERS = ("xyz", "yzx", "zxy")
MESH = pl.DeviceIdType.MESH
F32, BF16 = jnp.float32, jnp.bfloat16

BLOCKS = (
    (0, 0, 0, (256,)),
    (1, 0, 1, (256,)),
    (0, 256, 2, (256,)),
    (1, 256, 0, (256,)),
    (0, 512, 1, (256,)),
    (1, 512, 2, (256,)),
    (2, 0, 0, (256,)),
    (2, 256, 1, (256,)),
    (2, 512, 2, (256,)),
)
ORDER = (
    (0, 0, 0), (0, 1, 0), (0, 2, 0), (0, 0, 1), (0, 1, 1), (1, 0, 0), (0, 0, 2), (0, 3, 0),
    (1, 1, 0), (0, 3, 1), (0, 3, 2), (0, 4, 0), (0, 4, 1), (1, 2, 0), (0, 5, 0), (0, 6, 0),
    (0, 6, 1), (0, 6, 2), (0, 7, 0), (0, 7, 1), (0, 8, 0), (2, 0, 0), (2, 1, 0), (1, 3, 0),
    (2, 2, 0), (1, 4, 0), (1, 5, 0), (1, 6, 0), (1, 7, 0), (1, 8, 0), (1, 0, 1), (2, 3, 0),
    (1, 1, 1), (1, 2, 1), (2, 4, 0), (2, 5, 0), (2, 6, 0), (2, 7, 0), (2, 2, 1), (2, 0, 1),
    (1, 5, 1), (1, 3, 1), (2, 8, 0), (2, 1, 1), (1, 6, 1), (1, 4, 1), (2, 5, 1), (1, 2, 2),
    (1, 8, 1), (1, 7, 1), (2, 3, 1), (1, 1, 2), (1, 0, 2), (2, 6, 1), (1, 5, 2), (2, 2, 2),
    (2, 4, 1), (2, 8, 1), (2, 7, 1), (2, 1, 2), (1, 3, 2), (2, 5, 2), (2, 0, 2), (1, 6, 2),
    (1, 4, 2), (1, 8, 2), (1, 7, 2), (2, 3, 2), (2, 6, 2), (2, 4, 2), (2, 8, 2), (2, 7, 2),
)
CHUNKS = tuple(
    (b[0], b[1] + sum(b[3][:i]), w, DIM_ORDERS[b[2]]) for b in BLOCKS for i, w in enumerate(b[3]))
BLOCK_CHUNKS = tuple(
    tuple(sum(len(a[3]) for a in BLOCKS[:n]) + i for i in range(len(b[3]))) for n, b in enumerate(BLOCKS))
RAW = 256
PIECE = 32


def kernel(*refs):
    tokens, out_grad, gate_pre, up_pre, hidden_grad = refs[:5]
    outs = refs[5:8]
    tok, raw, hb = refs[8:11]
    n_chunk = len(CHUNKS)
    part = refs[11:11 + n_chunk]
    recv = tuple(refs[11 + (1 + ph) * n_chunk:11 + (2 + ph) * n_chunk] for ph in range(3))
    send_sem, recv_sem, in_sem, xs_sem, xr_sem = refs[11 + 4 * n_chunk:]

    z, yh, x, yl, c = (lax.axis_index(a) for a in AXES)
    y = yh * 2 + yl
    me = {"x": x, "y": y, "z": z}
    n_tok = tokens.shape[0]
    n_slot, tile = tok.shape[1], tok.shape[3]
    n_raw = raw.shape[0]
    rows = part[0].shape[3]
    step = {d: tuple(lax.rem(me[d] + k, 4) for k in range(4)) for d in "xyz"}

    def device(d, k):
        at = dict(me)
        at[d] = step[d][k]
        return (at["z"], lax.div(at["y"], 2), at["x"], lax.rem(at["y"], 2), c)

    partner = (z, yh, x, yl, 1 - c)

    def slot_at(slot):
        return lax.rem(x + 2 + lax.div(slot, 2), 4), lax.rem(yl + lax.rem(slot, 2), 2)

    raws = (gate_pre, up_pre, hidden_grad)
    bigs = (tokens, out_grad)

    def pieces(core):
        found = {}
        for j in range(n_raw):
            for i, ref in enumerate(raws):
                found[("raw", j, i)] = (ref.at[:, pl.ds(j * RAW, RAW)], lambda r, j=j, i=i: raw.at[j, i, r])
        for w, ref in enumerate(bigs):
            for s in range(n_slot):
                sx, sl = slot_at(s)
                at = pl.multiple_of((sx * 4 + sl * 2 + core) * tile, tile)
                found[("big", w, s)] = (ref.at[:, pl.ds(at, tile)], lambda r, w=w, s=s: tok.at[w, s, r])
        return found

    names = [("raw", 0, i) for i in range(3)] + [("big", 0, s) for s in range(n_slot)]
    names += [("raw", j, i) for j in range(1, n_raw) for i in range(3)] + [("big", 1, s) for s in range(n_slot)]
    mine, theirs = pieces(c), pieces(1 - c)
    own, swap = {}, {}
    for n, name in enumerate(names):
        src, dst = mine[name]
        own[name] = pltpu.make_async_copy(src, dst(pl.ds(0, n_tok)), in_sem.at[n])
        own[name].start()

    barrier = pltpu.get_barrier_semaphore()
    pl.semaphore_signal(barrier, inc=1, device_id=partner, device_id_type=MESH)
    for d in "xyz":
        for k in (1, 3):
            pl.semaphore_signal(barrier, inc=1, device_id=device(d, k), device_id_type=MESH)
    pl.semaphore_wait(barrier, 7)

    for n, name in enumerate(names):
        src, dst = theirs[name]
        swap[name] = pltpu.make_async_remote_copy(
            src, dst(pl.ds(n_tok, n_tok)), xs_sem.at[n], xr_sem.at[n], device_id=partner, device_id_type=MESH)
        swap[name].start()

    have = set()

    def need(name):
        if name not in have:
            have.add(name)
            own[name].wait()
            swap[name].wait_recv()

    def hidden(j):
        if ("hidden", j) in have:
            return
        have.add(("hidden", j))
        for i in range(3):
            need(("raw", j, i))

        def body(i, carry):
            at = pl.ds(pl.multiple_of(i * PIECE, PIECE), PIECE)
            cs = pl.ds(j * RAW, RAW)
            gate_val = raw[j, 0, at].astype(F32)
            up_val = raw[j, 1, at].astype(F32)
            grad_val = raw[j, 2, at].astype(F32)
            sig = jax.nn.sigmoid(gate_val)
            activated = gate_val * sig
            hb[2, at, cs] = (activated * up_val).astype(BF16)
            hb[1, at, cs] = (grad_val * activated).astype(BF16)
            hb[0, at, cs] = (grad_val * up_val * sig * (1.0 + gate_val * (1.0 - sig))).astype(BF16)
            return carry

        lax.fori_loop(0, 2 * n_tok // PIECE, body, 0)

    copies = {}

    def base(k, ph):
        ref = part[k]
        for d in CHUNKS[k][3][:ph]:
            ref = ref.at[me[d]]
        return ref

    def half_of(ref, i, h):
        n = ref.shape[1] // 2
        return ref.at[i, pl.ds(h * n, n)]

    def send(k, ph, i, src, direction):
        copies[(k, ph, i)] = pltpu.make_async_remote_copy(
            src, recv[ph][k].at[i], send_sem.at[k, ph, i], recv_sem.at[k, ph, i],
            device_id=device(CHUNKS[k][3][ph], direction), device_id_type=MESH)
        copies[(k, ph, i)].start()

    def send_far(k, ph):
        s = step[CHUNKS[k][3][ph]]
        send(k, ph, 0, half_of(base(k, ph), s[2], 0), 1)
        send(k, ph, 1, half_of(base(k, ph), s[2], 1), 3)

    def send_near(k, ph):
        s = step[CHUNKS[k][3][ph]]
        send(k, ph, 2, half_of(base(k, ph), s[1], 1), 1)
        send(k, ph, 3, half_of(base(k, ph), s[3], 0), 3)

    near = lambda i: 2 + 4 * lax.div(i, 2) + lax.rem(i, 2)
    parts_of = (
        ((2, lambda i: i), (4, near), (2, lambda i: 4 + i)),
        ((4, lambda i: 2 * i), (4, lambda i: 2 * i + 1)),
        ((n_slot, lambda i: i),),
    )
    slots_of = (
        ((0, 1), (2, 3, 6, 7), (4, 5)), ((0, 2, 4, 6), (1, 3, 5, 7)), (tuple(range(8)),))

    def multiply(b, seg):
        p, first, dim, widths = BLOCKS[b]
        w = p // 2
        for j in range(first // RAW, (first + sum(widths) - 1) // RAW + 1):
            hidden(j)
        for s in slots_of[dim][seg]:
            need(("big", w, s))
        count, slot_of = parts_of[dim][seg]

        def body(i, carry):
            slot = slot_of(i)
            res = lax.dot_general(
                tok[w, slot], hb[p, :, pl.ds(first, sum(widths))], (((0,), (0,)), ((), ())),
                preferred_element_type=F32).astype(BF16)
            sx, sl = slot_at(slot)
            for k in BLOCK_CHUNKS[b]:
                lane = CHUNKS[k][1] - first
                for sz in range(4):
                    for sh in range(2):
                        at = {"x": sx, "y": sh * 2 + sl, "z": sz}
                        lo = (sz * 2 + sh) * rows
                        o = CHUNKS[k][3]
                        part[k][at[o[0]], at[o[1]], at[o[2]]] = res[lo:lo + rows, lane:lane + CHUNKS[k][2]]
            return carry

        lax.fori_loop(0, count, body, 0)
        for k in BLOCK_CHUNKS[b]:
            if seg == 0:
                send_far(k, 0)
            if seg == 1 or len(parts_of[dim]) == 1:
                send_near(k, 0)

    def add(first, others, dst):
        lead = dst.shape[:-2]
        count = 1
        for n in lead:
            count *= n

        def block(ix):
            v = first[ix].astype(F32)
            for o in others:
                v = v + o[ix].astype(F32)
            dst[ix] = v.astype(dst.dtype)

        if not lead:
            block((slice(None), slice(None)))
            return

        def body(i, carry):
            block((i,) if len(lead) == 1 else (lax.div(i, lead[1]), lax.rem(i, lead[1])))
            return carry

        lax.fori_loop(0, count, body, 0)

    def relay(k, ph):
        s = step[CHUNKS[k][3][ph]]
        for i, to in ((0, 1), (1, 3)):
            copies[(k, ph, i)].wait_recv()
            got = recv[ph][k].at[i]
            add(got, (half_of(base(k, ph), s[to], i),), got)
            send(k, ph, 4 + i, got, to)

    def finish(k, ph):
        p, first, width, o = CHUNKS[k]
        got = recv[ph][k]
        for h, pair in enumerate(((3, 4), (2, 5))):
            for i in pair:
                copies[(k, ph, i)].wait_recv()
            own_half = half_of(base(k, ph), me[o[ph]], h)
            if ph < 2:
                dst = own_half
            else:
                dst = outs[p].at[pl.ds(h * (rows // 2), rows // 2), pl.ds(first, width)]
            add(own_half, tuple(got.at[i] for i in pair), dst)
        if ph < 2:
            send_far(k, ph + 1)
            send_near(k, ph + 1)

    for op, n, m in ORDER:
        (multiply, relay, finish)[op](n, m)

    for cp in swap.values():
        cp.wait_send()
    for cp in copies.values():
        cp.wait_send()


def on_device(tokens, out_grad, gate_pre, up_pre, hidden_grad):
    n_tok, width = tokens.shape
    hid = gate_pre.shape[1]
    rows = width // 128
    tile = width // 16
    dma = pltpu.SemaphoreType.DMA
    any_spec = pl.BlockSpec(memory_space=pl.ANY)
    vmem = pl.BlockSpec(memory_space=pltpu.VMEM)
    out = jax.ShapeDtypeStruct((rows, hid), F32)
    widths = [k[2] for k in CHUNKS]
    n_in = 3 * (hid // RAW) + 16
    return pl.pallas_call(
        kernel,
        out_shape=(out,) * 3,
        in_specs=[any_spec] * 5,
        out_specs=(vmem,) * 3,
        scratch_shapes=[
            pltpu.VMEM((2, 8, 2 * n_tok, tile), BF16),
            pltpu.VMEM((hid // RAW, 3, 2 * n_tok, RAW), BF16),
            pltpu.VMEM((3, 2 * n_tok, hid), BF16),
            *[pltpu.VMEM((4, 4, 4, rows, w), BF16) for w in widths],
            *[pltpu.VMEM((6, 2, 4, rows, w), BF16) for w in widths],
            *[pltpu.VMEM((6, 2, rows, w), BF16) for w in widths],
            *[pltpu.VMEM((6, rows // 2, w), BF16) for w in widths],
            dma((len(CHUNKS), 3, 6)),
            dma((len(CHUNKS), 3, 6)),
            dma((n_in,)),
            dma((n_in,)),
            dma((n_in,)),
        ],
        compiler_params=pltpu.CompilerParams(
            collective_id=0, has_side_effects=True, vmem_limit_bytes=67043328),
        name="grad_sum",
    )(tokens, out_grad, gate_pre, up_pre, hidden_grad)


def solution(mesh):
    split = Mesh(mesh.devices.reshape(4, 2, 4, 2, 2), AXES)
    spec_in = P(AXES, None)
    spec_out = P(("x", "yl", "c", "z", "yh"), None)
    return jax.shard_map(
        on_device, mesh=split, in_specs=(spec_in,) * 5, out_specs=(spec_out,) * 3, check_vma=False
    )
```

time: 482 us -> 101 us (0.21)
  waiting for transfers between devices: 262 us -> 0 us
  Pallas kernels: 0 us -> 95.3 us
  other arithmetic: 86.5 us -> 0 us
  matrix products: 64.7 us -> 0 us
  local copies, waits for them, and re-layouts: 33.5 us -> 4.85 us
  starting transfers between devices: 18.8 us -> 0 us
  between operations: 13.8 us -> 0.64 us
    all_gather x1 -> x0, waiting for transfers between devices: 106 us -> none  [in_one_piece(): lax.all_gather(both, axis, axis=dim, tiled=True)]
    all_to_all x2 -> x0, waiting for transfers between devices: 103 us -> none  [the longest x1 103 us: on_device(): lax.all_to_all(tokens, 'seq', split_axis=1, concat_axis=0, tiled=True)]
    pallas_call x0 -> x1, Pallas kernels: none -> 95.3 us  [on_device(): pl.pallas_call(kernel, out_shape=(out,) * 3, in_specs=[any_spec] * 5, out...]
    add x16 -> x0, other arithmetic: 76.9 us -> none  [add_shard(): total + lax.optimization_barrier(term.astype(jnp.bfloat16)).astype(jnp.fl...]
    dot_general x32 -> x0, matrix products: 64.7 us -> none  [contract_rows(): lax.dot_general(left, right, (((0,), (0,)), ((), ())), preferred_element_...]
    reduce_scatter x2 -> x0, waiting for transfers between devices: 53.7 us -> none  [scatter_axes(): x = lax.psum_scatter(x, axis, scatter_dimension=dim, tiled=True)]
    split x2 -> x0, local copies, waits for them, and re-layouts: 20.1 us -> none  [in_one_piece(): jnp.split(lax.all_gather(both, axis, axis=dim, tiled=True), ends, axis=al...]
    all_to_all x2 -> x0, starting transfers between devices: 18.7 us -> none  [the longest x1 13.1 us: on_device(): lax.all_to_all(out_grad, 'seq', split_axis=1, concat_axis=0, tiled=True)]
  transfers between devices with their start and end apart: 5 -> 0, of which waited for: 4 -> 0; matrix products, arithmetic and copies ran while one was open for 7% -> 0% of each run, Pallas kernels for 0% -> 0%
where the time goes in v2:
time: 101 us
  Pallas kernels  95.3 us (94%)
  local copies, waits for them, and re-layouts  4.85 us (5%)
    pallas_call x1, Pallas kernels, on_device(): pl.pallas_call(kernel, out_shape=(out,) * 3, in_specs=[any_spec] * 5, out...  95.3 us
    unnamed x3, local copies, waits for them, and re-layouts  4.85 us

profile of v2, /device:TPU:0, one launch (start us, length us, event | category | flops | bytes accessed | tf_op | source)
XLA Modules:
  0.0 100.8 jit_solution(12563203591505798657)
XLA Ops:
  0.6 95.3 %grad_sum.1 = (f32[64,768]{1,0:T(8,128)}, f32[64,768]{1,0:T(8,128)}, f32[64,768]{1,0:T(8,128)}) custom-call(bf16[320,8192]{1,0:T(8,128)(2,1)} %refs_0_.1, bf16[320,8192]{1,0:T(8,128)(2,1)} %refs_1_.1, bf16[320,768]{1,0:T(8,128)(2,1)} %refs_2_.1, bf16[320,768]{1,0:T(8,128)(2,1)} %refs_3_.1, bf16[320,768]{1,0:T(8,128)(2,1)} %refs_4_.1), custom_call_target="tpu_custom_call" | custom-call | tf_op jit(solution)/shard_map/grad_sum/pallas_call | solution.py:274
  95.9 1.6 %copy.11 = f32[64,768]{1,0:T(8,128)} copy(f32[64,768]{1,0:T(8,128)} %get-tuple-element.6) | data formatting | bytes 393216
  97.5 1.6 %copy.12 = f32[64,768]{1,0:T(8,128)} copy(f32[64,768]{1,0:T(8,128)} %get-tuple-element.7) | data formatting | bytes 393216
  99.1 1.6 %copy.13 = f32[64,768]{1,0:T(8,128)} copy(f32[64,768]{1,0:T(8,128)} %get-tuple-element.8) | data formatting | bytes 393216

commit v3 on v2

--- a/solution.py
+++ b/solution.py
@@ -7,7 +7,7 @@
 from jax.sharding import PartitionSpec as P
 
 AXES = ("z", "yh", "x", "yl", "c")
-DIM_ORDERS = ("xyz", "yzx", "zxy")
+DIM_ORDERS = ("xyz", "yzx", "zxy", "xzy", "yxz", "zyx")
 MESH = pl.DeviceIdType.MESH
 F32, BF16 = jnp.float32, jnp.bfloat16
 
@@ -23,22 +23,29 @@
     (2, 512, 2, (256,)),
 )
 ORDER = (
-    (0, 0, 0), (0, 1, 0), (0, 2, 0), (0, 0, 1), (0, 1, 1), (1, 0, 0), (0, 0, 2), (0, 3, 0),
-    (1, 1, 0), (0, 3, 1), (0, 3, 2), (0, 4, 0), (0, 4, 1), (1, 2, 0), (0, 5, 0), (0, 6, 0),
-    (0, 6, 1), (0, 6, 2), (0, 7, 0), (0, 7, 1), (0, 8, 0), (2, 0, 0), (2, 1, 0), (1, 3, 0),
-    (2, 2, 0), (1, 4, 0), (1, 5, 0), (1, 6, 0), (1, 7, 0), (1, 8, 0), (1, 0, 1), (2, 3, 0),
-    (1, 1, 1), (1, 2, 1), (2, 4, 0), (2, 5, 0), (2, 6, 0), (2, 7, 0), (2, 2, 1), (2, 0, 1),
-    (1, 5, 1), (1, 3, 1), (2, 8, 0), (2, 1, 1), (1, 6, 1), (1, 4, 1), (2, 5, 1), (1, 2, 2),
-    (1, 8, 1), (1, 7, 1), (2, 3, 1), (1, 1, 2), (1, 0, 2), (2, 6, 1), (1, 5, 2), (2, 2, 2),
-    (2, 4, 1), (2, 8, 1), (2, 7, 1), (2, 1, 2), (1, 3, 2), (2, 5, 2), (2, 0, 2), (1, 6, 2),
-    (1, 4, 2), (1, 8, 2), (1, 7, 2), (2, 3, 2), (2, 6, 2), (2, 4, 2), (2, 8, 2), (2, 7, 2),
+    (0, 3, 0), (3, 3, 0, 0), (0, 1, 0), (3, 1, 0, 0), (0, 2, 0), (3, 2, 0, 0), (0, 1, 1), (0, 6, 0),
+    (3, 1, 0, 1), (3, 2, 0, 1), (3, 6, 0, 0), (0, 4, 0), (0, 7, 0), (0, 3, 1), (1, 3, 0), (3, 4, 0, 0),
+    (1, 2, 0), (1, 1, 0), (0, 0, 0), (0, 8, 0), (3, 0, 0, 0), (3, 8, 0, 0), (0, 5, 0), (0, 4, 1),
+    (3, 3, 0, 1), (0, 6, 1), (3, 7, 0, 0), (3, 5, 0, 0), (0, 0, 1), (3, 6, 0, 1), (1, 6, 0), (3, 8, 0, 1),
+    (3, 5, 0, 1), (0, 7, 1), (1, 4, 0), (3, 7, 0, 1), (1, 0, 0), (1, 5, 0), (2, 1, 0), (3, 4, 0, 1),
+    (2, 2, 0), (1, 8, 0), (0, 3, 2), (3, 2, 1, 0), (3, 0, 0, 1), (3, 2, 1, 1), (1, 7, 0), (0, 0, 2),
+    (3, 1, 1, 0), (0, 6, 2), (2, 4, 0), (2, 3, 0), (2, 6, 0), (3, 6, 1, 0), (3, 3, 1, 1), (2, 5, 0),
+    (3, 1, 1, 1), (3, 3, 1, 0), (2, 7, 0), (3, 6, 1, 1), (3, 5, 1, 0), (1, 2, 1), (1, 6, 1), (2, 0, 0),
+    (3, 7, 1, 0), (2, 8, 0), (3, 4, 1, 0), (3, 0, 1, 0), (3, 8, 1, 0), (3, 7, 1, 1), (1, 1, 1), (3, 8, 1, 1),
+    (2, 2, 1), (3, 5, 1, 1), (3, 4, 1, 1), (1, 5, 1), (1, 3, 1), (3, 0, 1, 1), (1, 4, 1), (1, 0, 1),
+    (1, 7, 1), (3, 2, 2, 0), (1, 8, 1), (2, 6, 1), (2, 3, 1), (3, 3, 2, 0), (2, 5, 1), (3, 5, 2, 0),
+    (2, 1, 1), (3, 1, 2, 0), (3, 2, 2, 1), (2, 8, 1), (3, 8, 2, 0), (2, 0, 1), (3, 0, 2, 0), (2, 4, 1),
+    (3, 4, 2, 0), (1, 2, 2), (3, 6, 2, 0), (3, 1, 2, 1), (2, 7, 1), (3, 7, 2, 0), (3, 5, 2, 1), (1, 5, 2),
+    (3, 0, 2, 1), (3, 8, 2, 1), (3, 3, 2, 1), (1, 1, 2), (1, 3, 2), (3, 7, 2, 1), (3, 6, 2, 1), (3, 4, 2, 1),
+    (1, 8, 2), (1, 0, 2), (1, 4, 2), (2, 2, 2), (1, 6, 2), (1, 7, 2), (2, 5, 2), (2, 1, 2),
+    (2, 3, 2), (2, 8, 2), (2, 0, 2), (2, 6, 2), (2, 4, 2), (2, 7, 2),
 )
 CHUNKS = tuple(
     (b[0], b[1] + sum(b[3][:i]), w, DIM_ORDERS[b[2]]) for b in BLOCKS for i, w in enumerate(b[3]))
 BLOCK_CHUNKS = tuple(
     tuple(sum(len(a[3]) for a in BLOCKS[:n]) + i for i in range(len(b[3]))) for n, b in enumerate(BLOCKS))
 RAW = 256
-PIECE = 32
+PIECE = 64
 
 
 def kernel(*refs):
@@ -84,8 +91,8 @@
                 found[("big", w, s)] = (ref.at[:, pl.ds(at, tile)], lambda r, w=w, s=s: tok.at[w, s, r])
         return found
 
-    names = [("raw", 0, i) for i in range(3)] + [("big", 0, s) for s in range(n_slot)]
-    names += [("raw", j, i) for j in range(1, n_raw) for i in range(3)] + [("big", 1, s) for s in range(n_slot)]
+    names = [("raw", j, i) for j in range(2) for i in range(3)] + [("big", 0, s) for s in range(n_slot)]
+    names += [("raw", j, i) for j in range(2, n_raw) for i in range(3)] + [("big", 1, s) for s in range(n_slot)]
     mine, theirs = pieces(c), pieces(1 - c)
     own, swap = {}, {}
     for n, name in enumerate(names):
@@ -164,17 +171,17 @@
         send(k, ph, 2, half_of(base(k, ph), s[1], 1), 1)
         send(k, ph, 3, half_of(base(k, ph), s[3], 0), 3)
 
-    near = lambda i: 2 + 4 * lax.div(i, 2) + lax.rem(i, 2)
     parts_of = (
-        ((2, lambda i: i), (4, near), (2, lambda i: 4 + i)),
-        ((4, lambda i: 2 * i), (4, lambda i: 2 * i + 1)),
-        ((n_slot, lambda i: i),),
+        ((1, lambda i: (0, 1)), (2, lambda i: (2 + 4 * i, 3 + 4 * i)), (1, lambda i: (4, 5))),
+        ((2, lambda i: (4 * i, 4 * i + 2)), (2, lambda i: (4 * i + 1, 4 * i + 3))),
+        ((4, lambda i: (2 * i, 2 * i + 1)),),
     )
     slots_of = (
         ((0, 1), (2, 3, 6, 7), (4, 5)), ((0, 2, 4, 6), (1, 3, 5, 7)), (tuple(range(8)),))
 
     def multiply(b, seg):
         p, first, dim, widths = BLOCKS[b]
+        dim %= 3
         w = p // 2
         for j in range(first // RAW, (first + sum(widths) - 1) // RAW + 1):
             hidden(j)
@@ -183,27 +190,24 @@
         count, slot_of = parts_of[dim][seg]
 
         def body(i, carry):
-            slot = slot_of(i)
+            pair = slot_of(i)
+            left = jnp.concatenate([tok[w, s] for s in pair], axis=1)
             res = lax.dot_general(
-                tok[w, slot], hb[p, :, pl.ds(first, sum(widths))], (((0,), (0,)), ((), ())),
+                left, hb[p, :, pl.ds(first, sum(widths))], (((0,), (0,)), ((), ())),
                 preferred_element_type=F32).astype(BF16)
-            sx, sl = slot_at(slot)
-            for k in BLOCK_CHUNKS[b]:
-                lane = CHUNKS[k][1] - first
-                for sz in range(4):
-                    for sh in range(2):
-                        at = {"x": sx, "y": sh * 2 + sl, "z": sz}
-                        lo = (sz * 2 + sh) * rows
-                        o = CHUNKS[k][3]
-                        part[k][at[o[0]], at[o[1]], at[o[2]]] = res[lo:lo + rows, lane:lane + CHUNKS[k][2]]
+            for t, slot in enumerate(pair):
+                sx, sl = slot_at(slot)
+                for k in BLOCK_CHUNKS[b]:
+                    lane = CHUNKS[k][1] - first
+                    for sz in range(4):
+                        for sh in range(2):
+                            at = {"x": sx, "y": sh * 2 + sl, "z": sz}
+                            lo = t * tile + (sz * 2 + sh) * rows
+                            o = CHUNKS[k][3]
+                            part[k][at[o[0]], at[o[1]], at[o[2]]] = res[lo:lo + rows, lane:lane + CHUNKS[k][2]]
             return carry
 
         lax.fori_loop(0, count, body, 0)
-        for k in BLOCK_CHUNKS[b]:
-            if seg == 0:
-                send_far(k, 0)
-            if seg == 1 or len(parts_of[dim]) == 1:
-                send_near(k, 0)
 
     def add(first, others, dst):
         lead = dst.shape[:-2]
@@ -227,7 +231,16 @@
 
         lax.fori_loop(0, count, body, 0)
 
+    sent = set()
+
+    def sent_by(k, ph, which):
+        for i in which:
+            if ph >= 0 and (k, ph, i) not in sent:
+                sent.add((k, ph, i))
+                copies[(k, ph, i)].wait_send()
+
     def relay(k, ph):
+        sent_by(k, ph - 1, (4, 5))
         s = step[CHUNKS[k][3][ph]]
         for i, to in ((0, 1), (1, 3)):
             copies[(k, ph, i)].wait_recv()
@@ -235,7 +248,11 @@
             add(got, (half_of(base(k, ph), s[to], i),), got)
             send(k, ph, 4 + i, got, to)
 
+    def launch(k, ph, near_side):
+        (send_near if near_side else send_far)(k, ph)
+
     def finish(k, ph):
+        sent_by(k, ph, (0, 1, 2, 3))
         p, first, width, o = CHUNKS[k]
         got = recv[ph][k]
         for h, pair in enumerate(((3, 4), (2, 5))):
@@ -247,17 +264,20 @@
             else:
                 dst = outs[p].at[pl.ds(h * (rows // 2), rows // 2), pl.ds(first, width)]
             add(own_half, tuple(got.at[i] for i in pair), dst)
-        if ph < 2:
-            send_far(k, ph + 1)
-            send_near(k, ph + 1)
-
-    for op, n, m in ORDER:
-        (multiply, relay, finish)[op](n, m)
+
+    for op, n, m, *h in ORDER:
+        (multiply, relay, finish, launch)[op](n, m, *h)
 
     for cp in swap.values():
         cp.wait_send()
-    for cp in copies.values():
-        cp.wait_send()
+    for key, cp in copies.items():
+        if key not in sent:
+            cp.wait_send()
+
+
+def hand_out(*refs):
+    for src, dst in zip(refs[:3], refs[3:]):
+        dst[...] = src[...]
 
 
 def on_device(tokens, out_grad, gate_pre, up_pre, hidden_grad):
@@ -271,7 +291,7 @@
     out = jax.ShapeDtypeStruct((rows, hid), F32)
     widths = [k[2] for k in CHUNKS]
     n_in = 3 * (hid // RAW) + 16
-    return pl.pallas_call(
+    sums = pl.pallas_call(
         kernel,
         out_shape=(out,) * 3,
         in_specs=[any_spec] * 5,
@@ -294,6 +314,8 @@
             collective_id=0, has_side_effects=True, vmem_limit_bytes=67043328),
         name="grad_sum",
     )(tokens, out_grad, gate_pre, up_pre, hidden_grad)
+    return pl.pallas_call(
+        hand_out, out_shape=(out,) * 3, in_specs=[vmem] * 3, out_specs=(vmem,) * 3, name="hand_out")(*sums)
 
 
 def solution(mesh):

time: 101 us -> 95.2 us (0.943)
  local copies, waits for them, and re-layouts: 4.85 us -> 0 us
    unnamed x3 -> x0, local copies, waits for them, and re-layouts: 4.85 us -> none
    pallas_call x1, Pallas kernels: 95.3 us -> 92.4 us  [on_device(): pl.pallas_call(kernel, out_shape=(out,) * 3, in_specs=[any_spec] * 5, out...]
    pallas_call x0 -> x1, Pallas kernels: none -> 1.94 us  [on_device(): pl.pallas_call(hand_out, out_shape=(out,) * 3, in_specs=[vmem] * 3, out_s...]
where the time goes in v3:
time: 95.2 us; the launch traced here: 95 us
  Pallas kernels  94.4 us (99%)
    pallas_call x1, Pallas kernels, on_device(): pl.pallas_call(kernel, out_shape=(out,) * 3, in_specs=[any_spec] * 5, out...  92.4 us
    pallas_call x1, Pallas kernels, on_device(): pl.pallas_call(hand_out, out_shape=(out,) * 3, in_specs=[vmem] * 3, out_s...  1.94 us

profile of v3, /device:TPU:0, one launch (start us, length us, event | category | flops | bytes accessed | tf_op | source)
XLA Modules:
  0.0 95.0 jit_solution(10477186983541066040)
XLA Ops:
  0.6 92.4 %grad_sum.1 = (f32[64,768]{1,0:T(8,128)}, f32[64,768]{1,0:T(8,128)}, f32[64,768]{1,0:T(8,128)}) custom-call(bf16[320,8192]{1,0:T(8,128)(2,1)} %refs_0_.1, bf16[320,8192]{1,0:T(8,128)(2,1)} %refs_1_.1, bf16[320,768]{1,0:T(8,128)(2,1)} %refs_2_.1, bf16[320,768]{1,0:T(8,128)(2,1)} %refs_3_.1, bf16[320,768]{1,0:T(8,128)(2,1)} %refs_4_.1), custom_call_target="tpu_custom_call" | custom-call | tf_op jit(solution)/shard_map/grad_sum/pallas_call | solution.py:294
  93.1 1.9 %hand_out.1 = (f32[64,768]{1,0:T(8,128)}, f32[64,768]{1,0:T(8,128)}, f32[64,768]{1,0:T(8,128)}) custom-call(f32[64,768]{1,0:T(8,128)} %get-tuple-element.6.refs_0_, f32[64,768]{1,0:T(8,128)} %get-tuple-element.7.refs_1_, f32[64,768]{1,0:T(8,128)} %get-tuple-element.8.refs_2_), custom_call_target="tpu_custom_call" | custom-call | tf_op jit(solution)/shard_map/hand_out/pallas_call | solution.py:317

commit v4 on v3

v4 whole, which is shorter than its diff:
```python
import jax
import jax.numpy as jnp
from jax import lax
from jax.experimental import pallas as pl
from jax.experimental.pallas import tpu as pltpu
from jax.sharding import Mesh
from jax.sharding import PartitionSpec as P

AXES = ("z", "yh", "x", "yl", "c")
DIM_ORDERS = ("xyz", "yzx", "zxy", "xzy", "yxz", "zyx")
MESH = pl.DeviceIdType.MESH
F32, BF16 = jnp.float32, jnp.bfloat16

BLOCKS = (
    (0, 0, 2, (256,)),
    (1, 0, 0, (256,)),
    (0, 256, 1, (256,)),
    (1, 256, 2, (256,)),
    (0, 512, 0, (256,)),
    (1, 512, 1, (256,)),
    (2, 0, 2, (256,)),
    (2, 256, 0, (256,)),
    (2, 512, 1, (256,)),
)
ORDER = (
    (0, 0, 0), (3, 0, 0, 0), (0, 1, 0), (3, 1, 0, 0), (0, 2, 0), (3, 2, 0, 0), (0, 0, 1), (0, 3, 0),
    (0, 7, 0), (3, 3, 0, 0), (3, 7, 0, 0), (0, 1, 1), (3, 0, 0, 1), (0, 2, 1), (3, 2, 0, 1), (1, 0, 0),
    (0, 8, 0), (3, 8, 0, 0), (1, 1, 0), (3, 1, 0, 1), (0, 6, 0), (0, 7, 1), (0, 3, 1), (0, 1, 2),
    (0, 4, 0), (0, 4, 1), (3, 3, 0, 1), (1, 2, 0), (3, 6, 0, 0), (3, 4, 0, 0), (0, 6, 1), (0, 5, 0),
    (0, 7, 2), (0, 3, 2), (0, 0, 2), (3, 6, 0, 1), (3, 5, 0, 0), (1, 3, 0), (1, 7, 0), (3, 4, 0, 1),
    (2, 0, 0), (2, 1, 0), (3, 0, 1, 0), (0, 5, 1), (3, 1, 1, 0), (3, 5, 0, 1), (1, 4, 0), (0, 8, 1),
    (1, 5, 0), (1, 8, 0), (1, 6, 0), (3, 8, 0, 1), (2, 2, 0), (0, 4, 2), (3, 2, 1, 0), (3, 7, 0, 1),
    (3, 2, 1, 1), (2, 3, 0), (2, 5, 0), (2, 4, 0), (3, 3, 1, 0), (3, 4, 1, 0), (1, 1, 1), (0, 6, 2),
    (2, 6, 0), (3, 6, 1, 0), (3, 5, 1, 0), (1, 2, 1), (1, 0, 1), (3, 5, 1, 1), (3, 3, 1, 1), (3, 6, 1, 1),
    (2, 7, 0), (3, 4, 1, 1), (1, 3, 1), (2, 8, 0), (3, 8, 1, 0), (3, 8, 1, 1), (1, 6, 1), (3, 7, 1, 0),
    (1, 4, 1), (1, 5, 1), (2, 2, 1), (3, 1, 1, 1), (3, 0, 1, 1), (1, 8, 1), (3, 2, 2, 0), (3, 2, 2, 1),
    (3, 7, 1, 1), (1, 7, 1), (2, 5, 1), (2, 4, 1), (3, 5, 2, 0), (2, 6, 1), (3, 6, 2, 0), (3, 4, 2, 0),
    (2, 3, 1), (2, 1, 1), (3, 6, 2, 1), (3, 1, 2, 0), (3, 3, 2, 0), (2, 0, 1), (1, 2, 2), (2, 8, 1),
    (3, 0, 2, 0), (3, 8, 2, 0), (3, 4, 2, 1), (2, 7, 1), (3, 7, 2, 0), (3, 3, 2, 1), (1, 5, 2), (1, 6, 2),
    (1, 4, 2), (3, 5, 2, 1), (1, 3, 2), (3, 1, 2, 1), (3, 7, 2, 1), (3, 8, 2, 1), (2, 2, 2), (3, 0, 2, 1),
    (1, 8, 2), (1, 1, 2), (1, 0, 2), (1, 7, 2), (2, 6, 2), (2, 4, 2), (2, 3, 2), (2, 8, 2),
    (2, 5, 2), (2, 1, 2), (2, 0, 2), (2, 7, 2),
)
DIRECT = ()
CHUNKS = tuple(
    (b[0], b[1] + sum(b[3][:i]), w, DIM_ORDERS[b[2]]) for b in BLOCKS for i, w in enumerate(b[3]))
BLOCK_CHUNKS = tuple(
    tuple(sum(len(a[3]) for a in BLOCKS[:n]) + i for i in range(len(b[3]))) for n, b in enumerate(BLOCKS))
RAW = 256
PIECE = 64


def kernel(*refs):
    tokens, out_grad, gate_pre, up_pre, hidden_grad = refs[:5]
    outs = refs[5:8]
    tok, raw, hb = refs[8:11]
    n_chunk = len(CHUNKS)
    part = refs[11:11 + n_chunk]
    recv = tuple(refs[11 + (1 + ph) * n_chunk:11 + (2 + ph) * n_chunk] for ph in range(3))
    send_sem, recv_sem, in_sem, xs_sem, xr_sem, out_sem, result = refs[11 + 4 * n_chunk:]

    z, yh, x, yl, c = (lax.axis_index(a) for a in AXES)
    y = yh * 2 + yl
    me = {"x": x, "y": y, "z": z}
    n_tok = tokens.shape[0]
    n_slot, tile = tok.shape[1], tok.shape[3]
    n_raw = raw.shape[0]
    rows = part[0].shape[3]
    step = {d: tuple(lax.rem(me[d] + k, 4) for k in range(4)) for d in "xyz"}

    def device(d, k):
        at = dict(me)
        at[d] = step[d][k]
        return (at["z"], lax.div(at["y"], 2), at["x"], lax.rem(at["y"], 2), c)

    partner = (z, yh, x, yl, 1 - c)

    def slot_at(slot):
        return lax.rem(x + 2 + lax.div(slot, 2), 4), lax.rem(yl + lax.rem(slot, 2), 2)

    raws = (gate_pre, up_pre, hidden_grad)

    def pieces(core):
        found = {}
        for j in range(n_raw):
            for i, ref in enumerate(raws):
                found[("raw", j, i)] = (ref.at[:, pl.ds(j * RAW, RAW)], lambda r, j=j, i=i: raw.at[j, i, r])
        lanes = tile // 4
        for s in range(n_slot):
            sx, sl = slot_at(s)
            at = (sx * 4 + sl * 2 + core) * tile
            for k in range(4):
                src = tokens.at[:, pl.ds(pl.multiple_of(at + step["z"][k] * lanes, lanes), lanes)]
                cut = pl.ds(pl.multiple_of(step["z"][k] * lanes, lanes), lanes)
                found[("tok", s, k)] = (src, lambda r, s=s, cut=cut: tok.at[0, s, r, cut])
            src = out_grad.at[:, pl.ds(pl.multiple_of(at, tile), tile)]
            found[("grad", s)] = (src, lambda r, s=s: tok.at[1, s, r])
        return found

    def raw_names(j):
        return [("raw", j, i) for i in range(3)]

    def rest(slots):
        return [("tok", s, k) for s in slots for k in (0, 1, 3)]

    def grad_names(slots):
        return [("grad", s) for s in slots]

    def lanes_of(slots):
        return lambda r: tok.at[0, pl.ds(0, len(slots)), r, pl.ds(0, 3 * tile // 4)]

    def grads_of(slots):
        return lambda r: tok.at[1, pl.ds(0, len(slots)), r]

    def raw_of(j):
        return lambda r: raw.at[j, :, r]

    far_lanes = pl.ds(pl.multiple_of(step["z"][2] * (tile // 4), tile // 4), tile // 4)
    groups = [(raw_names(0), raw_of(0)),
              ([("tok", s, 2) for s in range(n_slot)], lambda r: tok.at[0, :, r, far_lanes]),
              (rest((0, 1)), lanes_of((0, 1))), (raw_names(1), raw_of(1)),
              (rest((2, 4, 6)), lanes_of((2, 4, 6))), (rest((3, 5, 7)), lanes_of((3, 5, 7)))]
    groups += [(raw_names(j), raw_of(j)) for j in range(2, n_raw)]
    groups += [(grad_names(s), grads_of(s)) for s in ((0, 1), (2, 3, 6, 7), (4, 5))]
    kinds = ("raw", "tok", "grad")
    whole = (lambda r: raw.at[:, :, r], lambda r: tok.at[0, :, r], lambda r: tok.at[1, :, r])
    first_rows, last_rows = pl.ds(0, n_tok), pl.ds(n_tok, n_tok)

    def take(ref, sem):
        pltpu.make_async_copy(ref, ref, sem).wait()

    mine, theirs = pieces(c), pieces(1 - c)
    for names, size in groups:
        for name in names:
            src, dst = mine[name]
            pltpu.make_async_copy(src, dst(first_rows), in_sem.at[kinds.index(name[0])]).start()

    barrier = pltpu.get_barrier_semaphore()
    pl.semaphore_signal(barrier, inc=1, device_id=partner, device_id_type=MESH)
    for d in "xyz":
        for k in (1, 2, 3):
            pl.semaphore_signal(barrier, inc=1, device_id=device(d, k), device_id_type=MESH)
    pl.semaphore_wait(barrier, 10)

    group_of = {}
    for n, (names, size) in enumerate(groups):
        for name in names:
            group_of[name] = n
            src, dst = theirs[name]
            pltpu.make_async_remote_copy(
                src, dst(last_rows), xs_sem.at[kinds.index(name[0])], xr_sem.at[n],
                device_id=partner, device_id_type=MESH).start()

    have = set()

    def need(name):
        kind = kinds.index(name[0])
        if name[0] not in have:
            have.add(name[0])
            take(whole[kind](first_rows), in_sem.at[kind])
        n = group_of[name]
        if n not in have:
            have.add(n)
            take(groups[n][1](last_rows), xr_sem.at[n])

    def hidden(j):
        if ("hidden", j) in have:
            return
        have.add(("hidden", j))
        for i in range(3):
            need(("raw", j, i))

        def body(i, carry):
            at = pl.ds(pl.multiple_of(i * PIECE, PIECE), PIECE)
            cs = pl.ds(j * RAW, RAW)
            gate_val = raw[j, 0, at].astype(F32)
            up_val = raw[j, 1, at].astype(F32)
            grad_val = raw[j, 2, at].astype(F32)
            sig = jax.nn.sigmoid(gate_val)
            activated = gate_val * sig
            hb[2, at, cs] = (activated * up_val).astype(BF16)
            hb[1, at, cs] = (grad_val * activated).astype(BF16)
            hb[0, at, cs] = (grad_val * up_val * sig * (1.0 + gate_val * (1.0 - sig))).astype(BF16)
            return carry

        lax.fori_loop(0, 2 * n_tok // PIECE, body, 0)

    def base(k, ph):
        ref = part[k]
        for d in CHUNKS[k][3][:ph]:
            ref = ref.at[me[d]]
        return ref

    def half_of(ref, i, h):
        n = ref.shape[1] // 2
        return ref.at[i, pl.ds(h * n, n)]

    def send(k, ph, i, src, direction):
        late = 1 if i > 1 or (k, ph) in DIRECT else 0
        pltpu.make_async_remote_copy(
            src, recv[ph][k].at[i], send_sem.at[k, ph], recv_sem.at[k, ph, late],
            device_id=device(CHUNKS[k][3][ph], direction), device_id_type=MESH).start()

    def launch(k, ph, near_side):
        s = step[CHUNKS[k][3][ph]]
        b = base(k, ph)
        if (k, ph) in DIRECT:
            for i, to in ((1, 1), (2, 3)) if near_side else ((0, 2),):
                send(k, ph, i, b.at[s[to]], to)
        elif near_side:
            send(k, ph, 2, half_of(b, s[1], 1), 1)
            send(k, ph, 3, half_of(b, s[3], 0), 3)
        else:
            send(k, ph, 0, half_of(b, s[2], 0), 1)
            send(k, ph, 1, half_of(b, s[2], 1), 3)

    slots_of = (((0, 1), (2, 3, 6, 7), (4, 5)), ((0, 2, 4, 6), (1, 3, 5, 7)), (range(8),) * 3)
    pairs_of = (
        ((1, lambda i: (0, 1)), (2, lambda i: (2 + 4 * i, 3 + 4 * i)), (1, lambda i: (4, 5))),
        ((2, lambda i: (4 * i, 4 * i + 2)), (2, lambda i: (4 * i + 1, 4 * i + 3))),
    )
    z_of = ((1, lambda i: 2), (2, lambda i: 1 + 2 * i), (1, lambda i: 0))

    def multiply(b, seg):
        p, first, dim, widths = BLOCKS[b]
        dim %= 3
        w = p // 2
        for j in range(first // RAW, (first + sum(widths) - 1) // RAW + 1):
            hidden(j)
        for s in slots_of[dim][seg]:
            if w:
                need(("grad", s))
            else:
                for k in ((2,), (1, 3), (0,))[seg] if dim == 2 else range(4):
                    need(("tok", s, k))
        count, which = (z_of if dim == 2 else pairs_of[dim])[seg]
        lanes = tile // 4

        def body(i, carry):
            if dim == 2:
                sz = lax.rem(z + which(i), 4)
                slots, levels = range(n_slot), (sz,)
                cut = pl.ds(pl.multiple_of(sz * lanes, lanes), lanes)
                left = [tok[w, s, :, cut] for s in slots]
            else:
                slots, levels = which(i), range(4)
                left = [tok[w, s] for s in slots]
            res = lax.dot_general(
                jnp.concatenate(left, axis=1), hb[p, :, pl.ds(first, sum(widths))], (((0,), (0,)), ((), ())),
                preferred_element_type=F32).astype(BF16)
            lo = 0
            for slot in slots:
                sx, sl = slot_at(slot)
                for sz in levels:
                    for sh in range(2):
                        at = {"x": sx, "y": sh * 2 + sl, "z": sz}
                        for k in BLOCK_CHUNKS[b]:
                            lane = CHUNKS[k][1] - first
                            o = CHUNKS[k][3]
                            part[k][at[o[0]], at[o[1]], at[o[2]]] = res[lo:lo + rows, lane:lane + CHUNKS[k][2]]
                        lo += rows
            return carry

        lax.fori_loop(0, count, body, 0)

    def add(first, others, dst):
        lead = dst.shape[:-2]
        count = 1
        for n in lead:
            count *= n

        def block(ix):
            v = first[ix].astype(F32)
            for o in others:
                v = v + o[ix].astype(F32)
            dst[ix] = v.astype(dst.dtype)

        if not lead:
            block((slice(None), slice(None)))
            return

        def body(i, carry):
            block((i,) if len(lead) == 1 else (lax.div(i, lead[1]), lax.rem(i, lead[1])))
            return carry

        lax.fori_loop(0, count, body, 0)

    def relay(k, ph):
        s = step[CHUNKS[k][3][ph]]
        take(recv[ph][k].at[pl.ds(0, 2)], recv_sem.at[k, ph, 0])
        for i, to in ((0, 1), (1, 3)):
            got = recv[ph][k].at[i]
            add(got, (half_of(base(k, ph), s[to], i),), got)
            send(k, ph, 4 + i, got, to)

    def finish(k, ph):
        p, first, width, o = CHUNKS[k]
        b, got, at = base(k, ph), recv[ph][k], me[o[ph]]
        cut = pl.ds(first, width)
        if (k, ph) in DIRECT:
            take(got, recv_sem.at[k, ph, 1])
            add(b.at[at], tuple(got.at[i] for i in range(3)), b.at[at] if ph < 2 else result.at[p, :, cut])
        else:
            take(got.at[pl.ds(2, 4)], recv_sem.at[k, ph, 1])
            for h, pair in enumerate(((3, 4), (2, 5))):
                own_half = half_of(b, at, h)
                n = rows // 2
                dst = own_half if ph < 2 else result.at[p, pl.ds(h * n, n), cut]
                add(own_half, tuple(got.at[i] for i in pair), dst)
        if ph == 2:
            pltpu.make_async_copy(result.at[p, :, cut], outs[p].at[:, cut], out_sem.at[0]).start()

    for op, n, m, *h in ORDER:
        (multiply, relay, finish, launch)[op](n, m, *h)

    for kind in range(3):
        take(whole[kind](first_rows), xs_sem.at[kind])
    for k in range(n_chunk):
        ref = part[k]
        for ph in range(3):
            take(ref.at[pl.ds(0, 3)], send_sem.at[k, ph])
            ref = ref.at[0]
    take(result, out_sem.at[0])


def hand_out(*refs):
    held, sem = refs[6:]
    into = [pltpu.make_async_copy(refs[p], held.at[p], sem.at[0, p]) for p in range(3)]
    back = [pltpu.make_async_copy(held.at[p], refs[3 + p], sem.at[1, p]) for p in range(3)]
    for cp in into:
        cp.start()
    for a, b in zip(into, back):
        a.wait()
        b.start()
    for cp in back:
        cp.wait()


def on_device(tokens, out_grad, gate_pre, up_pre, hidden_grad):
    n_tok, width = tokens.shape
    hid = gate_pre.shape[1]
    rows = width // 128
    tile = width // 16
    dma = pltpu.SemaphoreType.DMA
    any_spec = pl.BlockSpec(memory_space=pl.ANY)
    out = jax.ShapeDtypeStruct((rows, hid), F32)
    widths = [k[2] for k in CHUNKS]
    sums = pl.pallas_call(
        kernel,
        out_shape=(out,) * 3,
        in_specs=[any_spec] * 5,
        out_specs=(any_spec,) * 3,
        scratch_shapes=[
            pltpu.VMEM((2, 8, 2 * n_tok, tile), BF16),
            pltpu.VMEM((hid // RAW, 3, 2 * n_tok, RAW), BF16),
            pltpu.VMEM((3, 2 * n_tok, hid), BF16),
            *[pltpu.VMEM((4, 4, 4, rows, w), BF16) for w in widths],
            *[pltpu.VMEM((6, 2, 4, rows, w), BF16) for w in widths],
            *[pltpu.VMEM((3, 4, rows, w) if (k, 1) in DIRECT else (6, 2, rows, w), BF16) for k, w in enumerate(widths)],
            *[pltpu.VMEM((3, rows, w) if (k, 2) in DIRECT else (6, rows // 2, w), BF16) for k, w in enumerate(widths)],
            dma((len(CHUNKS), 3)),
            dma((len(CHUNKS), 3, 2)),
            dma((3,)),
            dma((3,)),
            dma((hid // RAW + 7,)),
            dma((1,)),
            pltpu.VMEM((3, rows, hid), F32),
        ],
        compiler_params=pltpu.CompilerParams(
            collective_id=0, has_side_effects=True, vmem_limit_bytes=67043328),
        name="grad_sum",
    )(tokens, out_grad, gate_pre, up_pre, hidden_grad)
    return pl.pallas_call(
        hand_out, out_shape=(out,) * 3, in_specs=[any_spec] * 3, out_specs=(any_spec,) * 3,
        scratch_shapes=[pltpu.VMEM((3, rows, hid), F32), dma((2, 3))], name="hand_out")(*sums)


def solution(mesh):
    split = Mesh(mesh.devices.reshape(4, 2, 4, 2, 2), AXES)
    spec_in = P(AXES, None)
    spec_out = P(("x", "yl", "c", "z", "yh"), None)
    return jax.shard_map(
        on_device, mesh=split, in_specs=(spec_in,) * 5, out_specs=(spec_out,) * 3, check_vma=False
    )
```

time: 95.2 us -> 90 us (0.945)
  Pallas kernels: 94.4 us -> 89 us
    pallas_call x1, Pallas kernels: 92.4 us -> 87.2 us  [on_device(): pl.pallas_call(kernel, out_shape=(out,) * 3, in_specs=[any_spec] * 5, out...]
where the time goes in v4:
time: 90 us; the launch traced here: 89.8 us
  Pallas kernels  89 us (99%)
    pallas_call x1, Pallas kernels, on_device(): pl.pallas_call(kernel, out_shape=(out,) * 3, in_specs=[any_spec] * 5, out...  87.2 us
    pallas_call x1, Pallas kernels, on_device(): pl.pallas_call(hand_out, out_shape=(out,) * 3, in_specs=[any_spec] * 3, o...  1.84 us

profile of v4, /device:TPU:0, one launch (start us, length us, event | category | flops | bytes accessed | tf_op | source)
XLA Modules:
  0.0 89.8 jit_solution(126191692856310892)
XLA Ops:
  0.6 87.2 %grad_sum.1 = (f32[64,768]{1,0:T(8,128)}, f32[64,768]{1,0:T(8,128)}, f32[64,768]{1,0:T(8,128)}) custom-call(bf16[320,8192]{1,0:T(8,128)(2,1)} %refs_0_.1, bf16[320,8192]{1,0:T(8,128)(2,1)} %refs_1_.1, bf16[320,768]{1,0:T(8,128)(2,1)} %refs_2_.1, bf16[320,768]{1,0:T(8,128)(2,1)} %refs_3_.1, bf16[320,768]{1,0:T(8,128)(2,1)} %refs_4_.1), custom_call_target="tpu_custom_call" | custom-call | tf_op jit(solution)/shard_map/grad_sum/pallas_call | solution.py:348
  87.8 1.8 %hand_out.1 = (f32[64,768]{1,0:T(8,128)}, f32[64,768]{1,0:T(8,128)}, f32[64,768]{1,0:T(8,128)}) custom-call(f32[64,768]{1,0:T(8,128)} %get-tuple-element.6.refs_0_, f32[64,768]{1,0:T(8,128)} %get-tuple-element.7.refs_1_, f32[64,768]{1,0:T(8,128)} %get-tuple-element.8.refs_2_), custom_call_target="tpu_custom_call" | custom-call | tf_op jit(solution)/shard_map/hand_out/pallas_call | solution.py:373

commit v5 on v4

--- a/solution.py
+++ b/solution.py
@@ -12,38 +12,39 @@
 F32, BF16 = jnp.float32, jnp.bfloat16
 
 BLOCKS = (
-    (0, 0, 2, (256,)),
-    (1, 0, 0, (256,)),
-    (0, 256, 1, (256,)),
-    (1, 256, 2, (256,)),
-    (0, 512, 0, (256,)),
-    (1, 512, 1, (256,)),
-    (2, 0, 2, (256,)),
-    (2, 256, 0, (256,)),
-    (2, 512, 1, (256,)),
+    (0, 0, (2,), (256,)),
+    (1, 0, (0,), (256,)),
+    (0, 256, (1,), (256,)),
+    (1, 256, (2,), (256,)),
+    (0, 512, (0, 3), (128, 128)),
+    (1, 512, (1,), (256,)),
+    (2, 0, (2,), (256,)),
+    (2, 256, (0,), (256,)),
+    (2, 512, (1,), (256,)),
 )
 ORDER = (
-    (0, 0, 0), (3, 0, 0, 0), (0, 1, 0), (3, 1, 0, 0), (0, 2, 0), (3, 2, 0, 0), (0, 0, 1), (0, 3, 0),
-    (0, 7, 0), (3, 3, 0, 0), (3, 7, 0, 0), (0, 1, 1), (3, 0, 0, 1), (0, 2, 1), (3, 2, 0, 1), (1, 0, 0),
-    (0, 8, 0), (3, 8, 0, 0), (1, 1, 0), (3, 1, 0, 1), (0, 6, 0), (0, 7, 1), (0, 3, 1), (0, 1, 2),
-    (0, 4, 0), (0, 4, 1), (3, 3, 0, 1), (1, 2, 0), (3, 6, 0, 0), (3, 4, 0, 0), (0, 6, 1), (0, 5, 0),
-    (0, 7, 2), (0, 3, 2), (0, 0, 2), (3, 6, 0, 1), (3, 5, 0, 0), (1, 3, 0), (1, 7, 0), (3, 4, 0, 1),
-    (2, 0, 0), (2, 1, 0), (3, 0, 1, 0), (0, 5, 1), (3, 1, 1, 0), (3, 5, 0, 1), (1, 4, 0), (0, 8, 1),
-    (1, 5, 0), (1, 8, 0), (1, 6, 0), (3, 8, 0, 1), (2, 2, 0), (0, 4, 2), (3, 2, 1, 0), (3, 7, 0, 1),
-    (3, 2, 1, 1), (2, 3, 0), (2, 5, 0), (2, 4, 0), (3, 3, 1, 0), (3, 4, 1, 0), (1, 1, 1), (0, 6, 2),
-    (2, 6, 0), (3, 6, 1, 0), (3, 5, 1, 0), (1, 2, 1), (1, 0, 1), (3, 5, 1, 1), (3, 3, 1, 1), (3, 6, 1, 1),
-    (2, 7, 0), (3, 4, 1, 1), (1, 3, 1), (2, 8, 0), (3, 8, 1, 0), (3, 8, 1, 1), (1, 6, 1), (3, 7, 1, 0),
-    (1, 4, 1), (1, 5, 1), (2, 2, 1), (3, 1, 1, 1), (3, 0, 1, 1), (1, 8, 1), (3, 2, 2, 0), (3, 2, 2, 1),
-    (3, 7, 1, 1), (1, 7, 1), (2, 5, 1), (2, 4, 1), (3, 5, 2, 0), (2, 6, 1), (3, 6, 2, 0), (3, 4, 2, 0),
-    (2, 3, 1), (2, 1, 1), (3, 6, 2, 1), (3, 1, 2, 0), (3, 3, 2, 0), (2, 0, 1), (1, 2, 2), (2, 8, 1),
-    (3, 0, 2, 0), (3, 8, 2, 0), (3, 4, 2, 1), (2, 7, 1), (3, 7, 2, 0), (3, 3, 2, 1), (1, 5, 2), (1, 6, 2),
-    (1, 4, 2), (3, 5, 2, 1), (1, 3, 2), (3, 1, 2, 1), (3, 7, 2, 1), (3, 8, 2, 1), (2, 2, 2), (3, 0, 2, 1),
-    (1, 8, 2), (1, 1, 2), (1, 0, 2), (1, 7, 2), (2, 6, 2), (2, 4, 2), (2, 3, 2), (2, 8, 2),
-    (2, 5, 2), (2, 1, 2), (2, 0, 2), (2, 7, 2),
+    (0, 0, 0), (3, 0, 0, 0), (0, 1, 0), (3, 1, 0, 0), (0, 3, 0), (3, 3, 0, 0), (0, 2, 0), (3, 2, 0, 0),
+    (0, 4, 0), (3, 5, 0, 0), (0, 4, 1), (0, 2, 1), (3, 4, 0, 1), (0, 0, 1), (3, 0, 0, 1), (3, 4, 0, 0),
+    (3, 2, 0, 1), (0, 8, 0), (0, 1, 1), (0, 3, 1), (1, 5, 0), (0, 6, 0), (1, 0, 0), (3, 9, 0, 0),
+    (0, 7, 0), (3, 7, 0, 0), (0, 8, 1), (3, 8, 0, 0), (1, 3, 0), (3, 9, 0, 1), (0, 0, 2), (0, 6, 1),
+    (0, 7, 1), (3, 5, 0, 1), (1, 4, 0), (0, 4, 2), (0, 5, 0), (3, 1, 0, 1), (1, 2, 0), (0, 3, 2),
+    (1, 8, 0), (0, 1, 2), (3, 6, 0, 0), (1, 9, 0), (3, 8, 0, 1), (2, 0, 0), (0, 5, 1), (3, 7, 0, 1),
+    (0, 7, 2), (2, 5, 0), (3, 5, 1, 0), (3, 3, 0, 1), (1, 1, 0), (1, 6, 0), (2, 4, 0), (3, 0, 1, 0),
+    (1, 7, 0), (3, 6, 0, 1), (0, 6, 2), (3, 4, 1, 0), (2, 3, 0), (2, 9, 0), (3, 3, 1, 0), (2, 2, 0),
+    (3, 2, 1, 0), (3, 4, 1, 1), (3, 3, 1, 1), (3, 9, 1, 1), (2, 8, 0), (3, 9, 1, 0), (2, 7, 0), (3, 7, 1, 0),
+    (3, 2, 1, 1), (2, 1, 0), (1, 5, 1), (3, 0, 1, 1), (3, 1, 1, 0), (3, 8, 1, 0), (2, 6, 0), (3, 6, 1, 0),
+    (3, 5, 1, 1), (3, 1, 1, 1), (1, 4, 1), (1, 2, 1), (1, 0, 1), (1, 9, 1), (1, 3, 1), (1, 7, 1),
+    (1, 1, 1), (3, 8, 1, 1), (3, 6, 1, 1), (3, 7, 1, 1), (2, 0, 1), (1, 8, 1), (2, 4, 1), (3, 0, 2, 0),
+    (3, 4, 2, 0), (1, 6, 1), (3, 0, 2, 1), (2, 2, 1), (3, 2, 2, 0), (2, 3, 1), (2, 5, 1), (2, 9, 1),
+    (3, 5, 2, 0), (3, 3, 2, 0), (3, 4, 2, 1), (3, 9, 2, 1), (3, 3, 2, 1), (3, 9, 2, 0), (2, 1, 1), (3, 1, 2, 0),
+    (3, 5, 2, 1), (2, 7, 1), (3, 7, 2, 0), (3, 1, 2, 1), (1, 4, 2), (1, 2, 2), (2, 8, 1), (3, 2, 2, 1),
+    (3, 8, 2, 0), (1, 0, 2), (3, 7, 2, 1), (2, 6, 1), (3, 6, 2, 0), (1, 1, 2), (3, 6, 2, 1), (3, 8, 2, 1),
+    (1, 5, 2), (1, 3, 2), (2, 4, 2), (2, 0, 2), (2, 9, 2), (2, 2, 2), (2, 1, 2), (2, 5, 2),
+    (2, 7, 2), (2, 3, 2), (2, 8, 2), (2, 6, 2),
 )
-DIRECT = ()
+DIRECT = ((6, 2), (7, 2), (8, 2), (9, 2))
 CHUNKS = tuple(
-    (b[0], b[1] + sum(b[3][:i]), w, DIM_ORDERS[b[2]]) for b in BLOCKS for i, w in enumerate(b[3]))
+    (b[0], b[1] + sum(b[3][:i]), w, DIM_ORDERS[b[2][i]]) for b in BLOCKS for i, w in enumerate(b[3]))
 BLOCK_CHUNKS = tuple(
     tuple(sum(len(a[3]) for a in BLOCKS[:n]) + i for i in range(len(b[3]))) for n, b in enumerate(BLOCKS))
 RAW = 256
@@ -223,7 +224,7 @@
 
     def multiply(b, seg):
         p, first, dim, widths = BLOCKS[b]
-        dim %= 3
+        dim = dim[0] % 3
         w = p // 2
         for j in range(first // RAW, (first + sum(widths) - 1) // RAW + 1):
             hidden(j)

time: 90 us -> 87.8 us (0.976)
  Pallas kernels: 89 us -> 86.2 us
    pallas_call x1, Pallas kernels: 87.2 us -> 84.3 us  [on_device(): pl.pallas_call(kernel, out_shape=(out,) * 3, in_specs=[any_spec] * 5, out...]
where the time goes in v5:
time: 87.8 us; the launch traced here: 87 us
  Pallas kernels  86.2 us (98%)
    pallas_call x1, Pallas kernels, on_device(): pl.pallas_call(kernel, out_shape=(out,) * 3, in_specs=[any_spec] * 5, out...  84.3 us
    pallas_call x1, Pallas kernels, on_device(): pl.pallas_call(hand_out, out_shape=(out,) * 3, in_specs=[any_spec] * 3, o...  1.84 us

profile of v5, /device:TPU:0, one launch (start us, length us, event | category | flops | bytes accessed | tf_op | source)
XLA Modules:
  0.0 87.0 jit_solution(6160713169796072258)
XLA Ops:
  0.6 84.3 %grad_sum.1 = (f32[64,768]{1,0:T(8,128)}, f32[64,768]{1,0:T(8,128)}, f32[64,768]{1,0:T(8,128)}) custom-call(bf16[320,8192]{1,0:T(8,128)(2,1)} %refs_0_.1, bf16[320,8192]{1,0:T(8,128)(2,1)} %refs_1_.1, bf16[320,768]{1,0:T(8,128)(2,1)} %refs_2_.1, bf16[320,768]{1,0:T(8,128)(2,1)} %refs_3_.1, bf16[320,768]{1,0:T(8,128)(2,1)} %refs_4_.1), custom_call_target="tpu_custom_call" | custom-call | tf_op jit(solution)/shard_map/grad_sum/pallas_call | solution.py:349
  85.0 1.8 %hand_out.1 = (f32[64,768]{1,0:T(8,128)}, f32[64,768]{1,0:T(8,128)}, f32[64,768]{1,0:T(8,128)}) custom-call(f32[64,768]{1,0:T(8,128)} %get-tuple-element.6.refs_0_, f32[64,768]{1,0:T(8,128)} %get-tuple-element.7.refs_1_, f32[64,768]{1,0:T(8,128)} %get-tuple-element.8.refs_2_), custom_call_target="tpu_custom_call" | custom-call | tf_op jit(solution)/shard_map/hand_out/pallas_call | solution.py:374

commit v6 on v5

--- a/solution.py
+++ b/solution.py
@@ -58,7 +58,7 @@
     n_chunk = len(CHUNKS)
     part = refs[11:11 + n_chunk]
     recv = tuple(refs[11 + (1 + ph) * n_chunk:11 + (2 + ph) * n_chunk] for ph in range(3))
-    send_sem, recv_sem, in_sem, xs_sem, xr_sem, out_sem, result = refs[11 + 4 * n_chunk:]
+    send_sem, recv_sem, in_sem, xs_sem, xr_sem = refs[11 + 4 * n_chunk:]
 
     z, yh, x, yl, c = (lax.axis_index(a) for a in AXES)
     y = yh * 2 + yl
@@ -300,16 +300,14 @@
         cut = pl.ds(first, width)
         if (k, ph) in DIRECT:
             take(got, recv_sem.at[k, ph, 1])
-            add(b.at[at], tuple(got.at[i] for i in range(3)), b.at[at] if ph < 2 else result.at[p, :, cut])
+            add(b.at[at], tuple(got.at[i] for i in range(3)), b.at[at] if ph < 2 else outs[p].at[:, cut])
         else:
             take(got.at[pl.ds(2, 4)], recv_sem.at[k, ph, 1])
             for h, pair in enumerate(((3, 4), (2, 5))):
                 own_half = half_of(b, at, h)
                 n = rows // 2
-                dst = own_half if ph < 2 else result.at[p, pl.ds(h * n, n), cut]
+                dst = own_half if ph < 2 else outs[p].at[pl.ds(h * n, n), cut]
                 add(own_half, tuple(got.at[i] for i in pair), dst)
-        if ph == 2:
-            pltpu.make_async_copy(result.at[p, :, cut], outs[p].at[:, cut], out_sem.at[0]).start()
 
     for op, n, m, *h in ORDER:
         (multiply, relay, finish, launch)[op](n, m, *h)
@@ -321,19 +319,13 @@
         for ph in range(3):
             take(ref.at[pl.ds(0, 3)], send_sem.at[k, ph])
             ref = ref.at[0]
-    take(result, out_sem.at[0])
 
 
 def hand_out(*refs):
-    held, sem = refs[6:]
-    into = [pltpu.make_async_copy(refs[p], held.at[p], sem.at[0, p]) for p in range(3)]
-    back = [pltpu.make_async_copy(held.at[p], refs[3 + p], sem.at[1, p]) for p in range(3)]
-    for cp in into:
+    copies = [pltpu.make_async_copy(refs[p], refs[3 + p], refs[6].at[p]) for p in range(3)]
+    for cp in copies:
         cp.start()
-    for a, b in zip(into, back):
-        a.wait()
-        b.start()
-    for cp in back:
+    for cp in copies:
         cp.wait()
 
 
@@ -344,13 +336,14 @@
     tile = width // 16
     dma = pltpu.SemaphoreType.DMA
     any_spec = pl.BlockSpec(memory_space=pl.ANY)
+    vmem = pl.BlockSpec(memory_space=pltpu.VMEM)
     out = jax.ShapeDtypeStruct((rows, hid), F32)
     widths = [k[2] for k in CHUNKS]
     sums = pl.pallas_call(
         kernel,
         out_shape=(out,) * 3,
         in_specs=[any_spec] * 5,
-        out_specs=(any_spec,) * 3,
+        out_specs=(vmem,) * 3,
         scratch_shapes=[
             pltpu.VMEM((2, 8, 2 * n_tok, tile), BF16),
             pltpu.VMEM((hid // RAW, 3, 2 * n_tok, RAW), BF16),
@@ -364,16 +357,15 @@
             dma((3,)),
             dma((3,)),
             dma((hid // RAW + 7,)),
-            dma((1,)),
-            pltpu.VMEM((3, rows, hid), F32),
         ],
         compiler_params=pltpu.CompilerParams(
-            collective_id=0, has_side_effects=True, vmem_limit_bytes=67043328),
+            collective_id=0, has_side_effects=True, vmem_limit_bytes=55850000),
         name="grad_sum",
     )(tokens, out_grad, gate_pre, up_pre, hidden_grad)
     return pl.pallas_call(
-        hand_out, out_shape=(out,) * 3, in_specs=[any_spec] * 3, out_specs=(any_spec,) * 3,
-        scratch_shapes=[pltpu.VMEM((3, rows, hid), F32), dma((2, 3))], name="hand_out")(*sums)
+        hand_out, out_shape=(out,) * 3, in_specs=[vmem] * 3, out_specs=(any_spec,) * 3,
+        scratch_shapes=[dma((3,))],
+        compiler_params=pltpu.CompilerParams(vmem_limit_bytes=1 << 20), name="hand_out")(*sums)
 
 
 def solution(mesh):

time: 87.8 us -> 86.2 us (0.982)
  Pallas kernels: 86.2 us -> 84.6 us
    pallas_call x1, Pallas kernels: 1.84 us -> 0.83 us  [on_device(): pl.pallas_call(hand_out, out_shape=(out,) * 3, in_specs=[vmem] * 3, out_s...]
where the time goes in v6:
time: 86.2 us; the launch traced here: 85.4 us
  Pallas kernels  84.6 us (98%)
    pallas_call x1, Pallas kernels, on_device(): pl.pallas_call(kernel, out_shape=(out,) * 3, in_specs=[any_spec] * 5, out...  83.7 us

profile of v6, /device:TPU:0, one launch (start us, length us, event | category | flops | bytes accessed | tf_op | source)
XLA Modules:
  0.0 85.4 jit_solution(11084560990603257051)
XLA Ops:
  0.6 83.7 %grad_sum.1 = (f32[64,768]{1,0:T(8,128)S(1)}, f32[64,768]{1,0:T(8,128)S(1)}, f32[64,768]{1,0:T(8,128)S(1)}) custom-call(bf16[320,8192]{1,0:T(8,128)(2,1)} %refs_0_.1, bf16[320,8192]{1,0:T(8,128)(2,1)} %refs_1_.1, bf16[320,768]{1,0:T(8,128)(2,1)} %refs_2_.1, bf16[320,768]{1,0:T(8,128)(2,1)} %refs_3_.1, bf16[320,768]{1,0:T(8,128)(2,1)} %refs_4_.1), custom_call_target="tpu_custom_call" | custom-call | tf_op jit(solution)/shard_map/grad_sum/pallas_call | solution.py:342
  84.4 0.8 hand_out.1

commit v7 on v6

--- a/solution.py
+++ b/solution.py
@@ -79,6 +79,12 @@
     def slot_at(slot):
         return lax.rem(x + 2 + lax.div(slot, 2), 4), lax.rem(yl + lax.rem(slot, 2), 2)
 
+    barrier = pltpu.get_barrier_semaphore()
+    pl.semaphore_signal(barrier, inc=1, device_id=partner, device_id_type=MESH)
+    for d in "xyz":
+        for k in (1, 2, 3):
+            pl.semaphore_signal(barrier, inc=1, device_id=device(d, k), device_id_type=MESH)
+
     raws = (gate_pre, up_pre, hidden_grad)
 
     def pieces(core):
@@ -94,6 +100,8 @@
                 src = tokens.at[:, pl.ds(pl.multiple_of(at + step["z"][k] * lanes, lanes), lanes)]
                 cut = pl.ds(pl.multiple_of(step["z"][k] * lanes, lanes), lanes)
                 found[("tok", s, k)] = (src, lambda r, s=s, cut=cut: tok.at[0, s, r, cut])
+            src = tokens.at[:, pl.ds(pl.multiple_of(at, tile), tile)]
+            found[("own", s)] = (src, lambda r, s=s: tok.at[0, s, r])
             src = out_grad.at[:, pl.ds(pl.multiple_of(at, tile), tile)]
             found[("grad", s)] = (src, lambda r, s=s: tok.at[1, s, r])
         return found
@@ -133,14 +141,13 @@
     mine, theirs = pieces(c), pieces(1 - c)
     for names, size in groups:
         for name in names:
-            src, dst = mine[name]
-            pltpu.make_async_copy(src, dst(first_rows), in_sem.at[kinds.index(name[0])]).start()
-
-    barrier = pltpu.get_barrier_semaphore()
-    pl.semaphore_signal(barrier, inc=1, device_id=partner, device_id_type=MESH)
-    for d in "xyz":
-        for k in (1, 2, 3):
-            pl.semaphore_signal(barrier, inc=1, device_id=device(d, k), device_id_type=MESH)
+            if name[0] != "tok":
+                src, dst = mine[name]
+                pltpu.make_async_copy(src, dst(first_rows), in_sem.at[kinds.index(name[0])]).start()
+            elif name[2] == 2:
+                src, dst = mine[("own", name[1])]
+                pltpu.make_async_copy(src, dst(first_rows), in_sem.at[1]).start()
+
     pl.semaphore_wait(barrier, 10)
 
     group_of = {}

time: 86.2 us -> 86 us (level)
  no operation moved by 1% of the time
where the time goes in v7:
time: 86 us; the launch traced here: 85.2 us
  Pallas kernels  84.4 us (98%)
    pallas_call x1, Pallas kernels, on_device(): pl.pallas_call(kernel, out_shape=(out,) * 3, in_specs=[any_spec] * 5, out...  83.6 us

profile of v7, /device:TPU:0, one launch (start us, length us, event | category | flops | bytes accessed | tf_op | source)
XLA Modules:
  0.0 85.2 jit_solution(7786133664250186349)
XLA Ops:
  0.6 83.6 %grad_sum.1 = (f32[64,768]{1,0:T(8,128)S(1)}, f32[64,768]{1,0:T(8,128)S(1)}, f32[64,768]{1,0:T(8,128)S(1)}) custom-call(bf16[320,8192]{1,0:T(8,128)(2,1)} %refs_0_.1, bf16[320,8192]{1,0:T(8,128)(2,1)} %refs_1_.1, bf16[320,768]{1,0:T(8,128)(2,1)} %refs_2_.1, bf16[320,768]{1,0:T(8,128)(2,1)} %refs_3_.1, bf16[320,768]{1,0:T(8,128)(2,1)} %refs_4_.1), custom_call_target="tpu_custom_call" | custom-call | tf_op jit(solution)/shard_map/grad_sum/pallas_call | solution.py:349
  84.2 0.8 hand_out.1
